TPU v7x, 32 devices: a whole 2x2x4 slice. The times are simulated.
32 devices in a mesh: lat: 4 (over z), lon: 8 (over y, x, core).
Axes of the slice: x: 2, y: 2, z: 4, core: 2. Of those that a mesh axis runs over, the one named last changes fastest.
Arguments:
- surface_forcing: float32 [4320, 1024], P('lon', 'lat'), may hold values from -40 to 40
- ocean_mask: int32 [4320, 1024], P('lon', 'lat'), may hold values 0 or 1
- self_coupling: float32 [4320, 1024], P('lon', 'lat'), may hold values from 0.2 to 2
- east_coupling: float32 [4320, 1024], P('lon', 'lat'), may hold values from 0.3 to 3
- north_coupling: float32 [4320, 1024], P('lon', 'lat'), may hold values from 0.3 to 3
- zonal_weight: float32 [1024], P('lat'), may hold values from 0.5 to 50
- aligned_inverse: float32 [8, 128, 128], P('lat'), may hold values from -1 to 4, as said below
- staggered_inverse: float32 [8, 128, 128], P('lat'), may hold values from -1 to 4, as said below
Outputs:
- solution: float32 [4320, 1024], P('lon', 'lat')
- residual: float32 [4320, 1024], P('lon', 'lat')
- direction: float32 [4320, 1024], P('lon', 'lat')
Inputs may be any that keep to these rules, and one draw needn't show every extreme that they name: `aligned_inverse`: each block is symmetric and positive definite. `staggered_inverse`: each block is symmetric and positive definite.
All inputs are finite; a program needn't handle non-finite values. No bound on the sum of `ocean_mask` on one device may be relied on, other than what follows from the above.
Results may differ from a plain program's by a relative error of at most 0.00023.
Values sent between devices are 32-bit elements; how exact they have to be, the bound alone decides.
A program may use at most 64 MiB of HBM per device.

v0:
```python
import functools

import jax
import jax.numpy as jnp
import numpy as np
from jax import lax
from jax.experimental import pallas as pl
from jax.experimental.pallas import tpu as pltpu
from jax.sharding import PartitionSpec as P

MESH = pl.DeviceIdType.MESH


def outer_table(groups):
    table = np.zeros((groups, groups))
    place = np.arange(groups)
    table[0] = 1.0
    table[1] = np.where(place % 2 == 0, 1.0, -1.0)
    for mode in range(1, groups // 2):
        turn = 2.0 * np.pi * (mode * place % groups) / groups
        table[2 * mode] = np.cos(turn)
        table[2 * mode + 1] = -np.sin(turn)
    table[np.abs(table) < 1e-12] = 0.0
    return table


def inner_tables(groups, length, padded):
    total = groups * length
    pairs = groups // 2
    matrix = np.zeros((pairs, 2 * padded, 2 * padded))
    waves = np.zeros((pairs, 2 * padded))
    cell = np.arange(length)

    def turns(modes):
        return 2.0 * np.pi * (modes[:, None] * cell[None, :] % total) / total

    def note(pair, start, modes):
        stop = start + len(modes)
        waves[pair, start:stop] = 2.0 - 2.0 * np.cos(2.0 * np.pi * modes / total)

    for part, (first, real_count) in enumerate(((0, length // 2 + 1), (groups // 2, (length + 1) // 2))):
        skipped = 1 if part == 0 else 0
        real = first + groups * np.arange(real_count)
        imag = first + groups * (skipped + np.arange(length - real_count))
        row = part * padded
        columns = slice(part * padded, part * padded + length)
        matrix[0, row : row + real_count, columns] = np.cos(turns(real))
        matrix[0, row + real_count : row + length, columns] = -np.sin(turns(imag))
        note(0, row, real)
        note(0, row + real_count, imag)
    for pair in range(1, pairs):
        modes = pair + groups * np.arange(length)
        angle = turns(modes)
        low, high = slice(0, length), slice(padded, padded + length)
        matrix[pair, low, low] = np.cos(angle)
        matrix[pair, low, high] = np.sin(angle)
        matrix[pair, high, low] = -np.sin(angle)
        matrix[pair, high, high] = np.cos(angle)
        note(pair, 0, modes)
        note(pair, padded, modes)
    single = matrix.astype(np.float32)
    leading = single.astype(jnp.bfloat16)
    rest = (matrix - leading.astype(np.float64)).astype(jnp.bfloat16)
    return np.stack([leading, rest], axis=1), waves.astype(np.float32)


def parted(value):
    leading = value.astype(jnp.bfloat16)
    return leading, (value - leading.astype(jnp.float32)).astype(jnp.bfloat16)


def dot(left, right):
    return jnp.dot(left, right, preferred_element_type=jnp.float32)


def weighted(values, factors):
    total = None
    for value, factor in zip(values, factors):
        if factor == 0.0:
            continue
        term = value if factor == 1.0 else value * np.float32(factor)
        total = term if total is None else total + term
    return total


class Plan:
    def __init__(self, groups, bands, length, columns, block, width_of):
        self.groups, self.bands, self.length = groups, bands, length
        self.pairs = groups // 2
        self.columns, self.block = columns, block
        self.chunk, self.padded = width_of
        self.width = 2 * self.padded
        self.rows = max(-(-length // 128) * 128, -(-self.padded // 128) * 128)
        self.tile = next(t for t in (384, 256, 128) if self.width % t == 0)
        self.table = outer_table(groups)

    def scratch(self):
        f32, bf16 = jnp.float32, jnp.bfloat16
        G, NP, C, PD, W, R, L = (
            self.groups, self.pairs, self.chunk, self.padded, self.width, self.rows, self.block
        )
        vmem, dma = pltpu.VMEM, pltpu.SemaphoreType.DMA
        return {
            "forcing": vmem((self.length, 2 * L), f32),
            "mask": vmem((self.length, 2 * L), jnp.int32),
            "selfc": vmem((self.length, 2 * L), f32),
            "eastc": vmem((self.length, 2 * L), f32),
            "northc": vmem((self.length, 2 * L), f32),
            "zonal": vmem((1, 2 * L), f32),
            "zonal_in": vmem((2, 1, 2 * L), f32),
            "aligned": vmem((2, L, L), f32),
            "staggered": vmem((2, L, L), f32),
            "carried": vmem((L, L), f32),
            "matrix": vmem((2, W, W), bf16),
            "turned": vmem((2, W, W), bf16),
            "wave": vmem((W, L), f32),
            "wet": vmem((2, R + 16, L), f32),
            "east_wet": vmem((2, R, L), f32),
            "east": vmem((2, R + 16, L), f32),
            "north": vmem((2, R, L), f32),
            "south": vmem((2, R, L), f32),
            "diag": vmem((2, R, L), f32),
            "field": vmem((2, R + 16, L), f32),
            "row_in": vmem((3, 2, 8, L), f32),
            "row_out": vmem((3, 2, 8, L), f32),
            "edge_out": vmem((2, 2, 8, L), f32),
            "edge_in": vmem((2, 2, 8, L), f32),
            "scale": vmem((3, W, L), f32),
            "scale_out": vmem((W, L), f32),
            "gain": vmem((2, 2 * L, L), bf16),
            "gain_z": vmem((2, L, L), bf16),
            "xs": vmem((2, 2, R, L), f32),
            "got1": vmem((2, 2, G, C, L), f32),
            "send2": vmem((2, NP, 2, 2, C, L), f32),
            "got2": vmem((2, 2, PD, L), f32),
            "mate2": vmem((2, 2, PD, L), f32),
            "zs": vmem((2, 2, PD, L), f32),
            "zgot": vmem((2, 2, PD, L), f32),
            "spec": vmem((2, W, L), f32),
            "spec_mate": vmem((W, L), f32),
            "spec_z": vmem((W, L), f32),
            "mixed": vmem((2, W, L), f32),
            "send3": vmem((2, 2, PD, L), f32),
            "got3": vmem((2, G, 2, C, L), f32),
            "send4": vmem((2, G, 2, C, L), f32),
            "got4": vmem((2, 2, R, L), f32),
            "ew": vmem((2, 2, 8, L), f32),
            "part": vmem((2, 2, 8, L), f32),
            "red1": vmem((2, G, 2, 8, L), f32),
            "middle": vmem((2, 2, 8, L), f32),
            "red2": vmem((2, self.bands, 2, 8, L), f32),
            "out": vmem((3, self.length, 2 * L), f32),
            "load": dma((16,)),
            "s1": dma((2, 2, NP, 2)),
            "r1": dma((2, 2, NP, 2)),
            "s2": dma((2, 2, NP, 2)),
            "r2": dma((2, NP, 2)),
            "sm": dma((2, NP, 2)),
            "rm": dma((2, NP, 2)),
            "sz": dma((2, 2, NP, 2)),
            "rz": dma((2, 2, NP, 2)),
            "s3": dma((2, NP, 2)),
            "r3": dma((2, NP, 2)),
            "s4": dma((2, 2, NP, 2)),
            "r4": dma((2, 2, NP, 2)),
            "sw": dma((2, 2, NP, 2)),
            "rw": dma((2, 2)),
            "srow": dma((3, 2)),
            "rrow": dma((3, 2)),
            "sedge": dma((2, 2)),
            "redge": dma((2, 2)),
            "szon": dma((2,)),
            "rzon": dma((2,)),
            "sstag": dma,
            "rstag": dma,
            "sa": dma((2, NP, 2)),
            "ra": dma((2, NP, 2)),
            "sb": dma((2, self.bands)),
            "rb": dma((2, self.bands)),
            "store": dma((3,)),
        }


class Refs:
    pass


def kernel(plan, names, *refs):
    (forcing_ref, mask_ref, self_ref, east_ref, north_ref, zonal_ref, aligned_ref, staggered_ref,
     matrix_ref, wave_ref, solution_ref, residual_ref, direction_ref) = refs[:13]
    s = Refs()
    for name, ref in zip(names, refs[13:]):
        setattr(s, name, ref)
    G, NP, C, PD, W, R, L = (
        plan.groups, plan.pairs, plan.chunk, plan.padded, plan.width, plan.rows, plan.block
    )
    bands, length, tile, table = plan.bands, plan.length, plan.tile, plan.table
    half = L // 2
    total = G * length
    f32 = jnp.float32
    band = lax.axis_index("lat")
    me = lax.axis_index("lon")
    pair, core = me // 2, me % 2
    mate = me + 1 - 2 * core
    has_up, has_down = band < bands - 1, band > 0
    STEPS = [(d, e) for d in range(1, NP) for e in (0, 1)] + [(0, 1)]
    last_chunk = (length - 1) // C
    last_tile = (length - 1) // 8 * 8
    last_row = (length - 1) % 8

    def to_dev(d, e):
        return 2 * ((pair + d) % NP) + (core + e) % 2

    def from_dev(d, e):
        return 2 * ((pair - d + NP) % NP) + (core + e) % 2

    def remote(src, dst, send, recv, device):
        return pltpu.make_async_remote_copy(
            src_ref=src, dst_ref=dst, send_sem=send, recv_sem=recv,
            device_id=device, device_id_type=MESH,
        )

    pending = []

    def launch(make, when=None):
        if when is None:
            make().start()
        else:
            pl.when(when)(lambda: make().start())
        pending.append((make, when))

    def await_recv(make, when=None):
        if when is None:
            make().wait_recv()
        else:
            pl.when(when)(lambda: make().wait_recv())

    def rows(index):
        return pl.ds(pl.multiple_of(index * C, 8), C)

    def span(index, size=128):
        return pl.ds(pl.multiple_of(index * size, size), size)

    def loop(count, body):
        def step(index, carry):
            body(index)
            return carry
        lax.fori_loop(0, count, step, 0)

    def eight_on(start, count):
        return pl.ds(start + 8 if isinstance(start, int) else pl.multiple_of(start + 8, 8), count)

    def loop_rows(body):
        full = length // 128
        loop(full, lambda index: body(pl.multiple_of(index * 128, 128), 128))
        if length % 128:
            body(full * 128, length % 128)

    def lanes_left(count):
        return lax.broadcasted_iota(jnp.int32, (count, L), 1) < half

    def groups_of(t0, t1):
        mask = lanes_left(t0.shape[0])
        return jnp.where(mask, t1, t0), jnp.where(mask, t0, t1)

    loads = []
    for index, (src, dst) in enumerate((
        (forcing_ref, s.forcing),
        (mask_ref, s.mask),
        (matrix_ref.at[pair], s.matrix),
        (wave_ref.at[pair], s.wave),
        (self_ref, s.selfc),
        (east_ref, s.eastc),
        (north_ref, s.northc),
        (zonal_ref, s.zonal),
        (aligned_ref, s.aligned),
        (staggered_ref, s.staggered),
    )):
        loads.append(pltpu.make_async_copy(src, dst, s.load.at[index]))
        loads[-1].start()

    barrier = pltpu.get_barrier_semaphore()
    for d, e in STEPS:
        pl.semaphore_signal(barrier, inc=1, device_id=(band, to_dev(d, e)), device_id_type=MESH)
    for step in range(1, bands):
        pl.semaphore_signal(
            barrier, inc=1, device_id=((band + step) % bands, me), device_id_type=MESH
        )

    loads[0].wait()
    loads[1].wait()
    s.xs[0, :, length:R, :] = jnp.zeros((2, R - length, L), f32)
    s.wet[:, 8 + length : 16 + R, :] = jnp.zeros((2, R + 8 - length, L), f32)
    s.field[:, 8 + R : 16 + R, :] = jnp.zeros((2, 8, L), f32)

    def make_rhs(start, count):
        at = pl.ds(start, count)
        wet = s.mask[at, :].astype(f32)
        rhs = wet * s.forcing[at, :]
        a, b = groups_of(rhs[:, :L], rhs[:, L:])
        s.xs[0, 0, at, :] = a
        s.xs[0, 1, at, :] = b
        at8 = eight_on(start, count)
        s.wet[0, at8, :] = wet[:, :L]
        s.wet[1, at8, :] = wet[:, L:]

    loop_rows(make_rhs)
    pl.semaphore_wait(barrier, G + bands - 2)

    def send_phase1(t, g):
        for d, e in STEPS:
            launch(functools.partial(
                lambda d, e: remote(
                    s.xs.at[t, g, rows(to_dev(d, e))], s.got1.at[t, g, me],
                    s.s1.at[t, g, d, e], s.r1.at[t, g, d, e], (band, to_dev(d, e))), d, e))
        s.got1[t, g, me] = s.xs[t, g, rows(me), :]

    def outer_forward(t, g):
        for d, e in STEPS:
            origin = from_dev(d, e)
            remote(s.xs.at[t, g, rows(origin)], s.got1.at[t, g, origin],
                   s.s1.at[t, g, d, e], s.r1.at[t, g, d, e], (band, origin)).wait_recv()

        def step(index):
            at = span(index, 8)
            values = [s.got1[t, g, place, at, :] for place in range(G)]
            for row in range(G):
                s.send2[t, row // 2, g, row % 2, at, :] = weighted(values, table[row])

        loop(C // 8, step)
        e = (g + core) % 2
        for d in list(range(1, NP)) + [0]:
            target = 2 * ((pair + d) % NP) + g
            launch(functools.partial(
                lambda d, target: remote(
                    s.send2.at[t, (pair + d) % NP, g], s.got2.at[t, :, rows(me), :],
                    s.s2.at[t, g, d, e], s.r2.at[t, d, e], (band, target)), d, target),
                None if d else core != g)

        @pl.when(core == g)
        def _():
            s.got2[t, :, rows(me), :] = s.send2[t, pair, g]

    def forward_on(t, d, e):
        origin = from_dev(d, e)
        at = rows(origin)
        launch(functools.partial(
            lambda at, d, e: remote(
                s.got2.at[t, :, at, :], s.mate2.at[t, :, at, :],
                s.sm.at[t, d, e], s.rm.at[t, d, e], (band, mate)), at, d, e))

        @pl.when(core == 1)
        def _():
            low, high = s.got2[t, 0, at, :], s.got2[t, 1, at, :]
            mask = lanes_left(C)
            s.zs[t, 0, at, :] = jnp.where(mask, low, pltpu.roll(high, half, 1))
            s.zs[t, 1, at, :] = jnp.where(mask, pltpu.roll(low, half, 1), high)

        launch(functools.partial(
            lambda at, d, e: remote(
                s.zs.at[t, 0, at, :], s.zgot.at[t, 0, at, :],
                s.sz.at[t, 0, d, e], s.rz.at[t, 0, d, e], (band - 1, me)), at, d, e),
            (core == 1) & has_down)
        launch(functools.partial(
            lambda at, d, e: remote(
                s.zs.at[t, 1, at, :], s.zgot.at[t, 1, at, :],
                s.sz.at[t, 1, d, e], s.rz.at[t, 1, d, e], (band + 1, me)), at, d, e),
            (core == 1) & has_up)

    def relay(t):
        forward_on(t, 0, 0)
        for d, e in [(0, 1)] + [step for step in STEPS if step[0]]:
            origin = from_dev(d, e)
            remote(s.send2.at[t, 0, 0], s.got2.at[t, :, rows(origin), :],
                   s.s2.at[t, 0, d, e], s.r2.at[t, d, e], (band, origin)).wait_recv()
            forward_on(t, d, e)

    def wait_mate(t):
        for d, e in [(0, 0)] + STEPS:
            at = rows(2 * ((pair - d + NP) % NP) + (1 - core + e) % 2)
            remote(s.got2.at[t, :, at, :], s.mate2.at[t, :, at, :],
                   s.sm.at[t, d, e], s.rm.at[t, d, e], (band, mate)).wait_recv()

    def transform(source, scale, put):
        hi, lo = parted(source)
        both = jnp.concatenate([hi, lo], axis=1)

        def step(index):
            at = span(index, tile)
            wide = dot(s.matrix[0, at, :], both)
            value = wide[:, :L] + (wide[:, L:] + dot(s.matrix[1, at, :], hi))
            put(at, value * scale[at, :])

        loop(W // tile, step)

    def put_in(ref):
        def put(at, value):
            ref[at, :] = value
        return put

    def own_spectrum(t):
        transform(s.got2[t].reshape(W, L), s.scale.at[0], put_in(s.spec.at[t]))

    def mate_spectrum(t):
        transform(s.mate2[t].reshape(W, L), s.scale.at[1], put_in(s.spec_mate))

    def mix(t):
        def step(index):
            at = span(index, tile)
            hi, lo = parted(jnp.concatenate([s.spec[t, at, :], s.spec_mate[at, :]], axis=1))
            s.mixed[t, at, :] = dot(hi, s.gain[0]) + (dot(lo, s.gain[0]) + dot(hi, s.gain[1]))

        loop(W // tile, step)

        @pl.when(core == 1)
        def _():
            for d, e in [(0, 0)] + STEPS:
                for way, has in ((0, has_up), (1, has_down)):
                    def wait(way=way, d=d, e=e):
                        at = rows(from_dev(d, e))
                        remote(s.zs.at[t, way, at, :], s.zgot.at[t, way, at, :],
                               s.sz.at[t, way, d, e], s.rz.at[t, way, d, e],
                               (band + 1 - 2 * way, me)).wait_recv()
                    pl.when(has)(wait)
            above, below = s.zgot[t, 0], s.zgot[t, 1]
            mask = lanes_left(PD)
            cells = jnp.concatenate([
                jnp.where(mask, above, pltpu.roll(below, half, 1)),
                jnp.where(mask, pltpu.roll(above, half, 1), below)], axis=0)

            def put(at, value):
                hi, lo = parted(value)
                s.mixed[t, at, :] = s.mixed[t, at, :] + (
                    dot(hi, s.gain_z[0]) + (dot(lo, s.gain_z[0]) + dot(hi, s.gain_z[1])))

            transform(cells, s.scale.at[2], put)

    def inner_back(t):
        hi, lo = parted(s.mixed[t] * s.scale_out[...])
        both = jnp.concatenate([hi, lo], axis=1)
        size = G // 2 * C
        first = 1 - me // (G // 2)
        for turn in range(2):
            side = first if turn == 0 else 1 - first
            for part in range(2):
                at = pl.ds(pl.multiple_of(part * PD + side * size, 16), size)
                wide = dot(s.turned[0, at, :], both)
                s.send3[t, part, pl.ds(pl.multiple_of(side * size, 8), size), :] = (
                    wide[:, :L] + (wide[:, L:] + dot(s.turned[1, at, :], hi)))
            for d, e in STEPS:
                to = to_dev(d, e)
                launch(functools.partial(
                    lambda d, e, to: remote(
                        s.send3.at[t, :, rows(to), :], s.got3.at[t, me],
                        s.s3.at[t, d, e], s.r3.at[t, d, e], (band, to)), d, e, to),
                    to // (G // 2) == side)
        s.got3[t, me] = s.send3[t, :, rows(me), :]

    def outer_back(t, g, edges):
        e = (g + core) % 2
        for d in range(NP):
            origin = 2 * ((pair - d + NP) % NP) + g
            await_recv(functools.partial(
                lambda d, origin: remote(
                    s.send3.at[t, :, rows(0), :], s.got3.at[t, origin],
                    s.s3.at[t, d, e], s.r3.at[t, d, e], (band, origin)), d, origin),
                None if d else core != g)

        def step(index):
            at = span(index, 8)
            values = [s.got3[t, 2 * (row // 2) + g, row % 2, at, :] for row in range(G)]
            for place in range(G):
                s.send4[t, place, g, at, :] = weighted(values, table[:, place])

        loop(C // 8, step)
        for d, e in STEPS:
            launch(functools.partial(
                lambda d, e: remote(
                    s.send4.at[t, to_dev(d, e), g], s.got4.at[t, g, rows(me), :],
                    s.s4.at[t, g, d, e], s.r4.at[t, g, d, e], (band, to_dev(d, e))), d, e))
        s.got4[t, g, rows(me), :] = s.send4[t, me, g]
        if not edges:
            return
        for way, (owner, shift, at) in enumerate((
            (0, 1, 0), (last_chunk, G - 1, (length - 1) % C // 8 * 8))):
            for d, e in STEPS:
                launch(functools.partial(
                    lambda way, shift, at, d, e: remote(
                        s.send4.at[t, (to_dev(d, e) + shift) % G, g, pl.ds(at, 8), :], s.ew.at[way, g],
                        s.sw.at[way, g, d, e], s.rw.at[way, g], (band, to_dev(d, e))),
                    way, shift, at, d, e), me == owner)

            @pl.when(me == owner)
            def _(way=way, shift=shift, at=at):
                s.ew[way, g] = s.send4[t, (me + shift) % G, g, pl.ds(at, 8), :]

    def wait_back(t, g, edges):
        for d, e in STEPS:
            origin = from_dev(d, e)
            remote(s.send4.at[t, 0, g], s.got4.at[t, g, rows(origin), :],
                   s.s4.at[t, g, d, e], s.r4.at[t, g, d, e], (band, origin)).wait_recv()
        if edges:
            for way, owner in enumerate((0, last_chunk)):
                await_recv(functools.partial(
                    lambda way: remote(
                        s.send4.at[t, 0, g, pl.ds(0, 8), :], s.ew.at[way, g],
                        s.sw.at[way, g, 0, 1], s.rw.at[way, g], (band, mate)), way), me != owner)

    def send_edges(i):
        for way, (device, has) in enumerate((((band - 1, me), has_down), ((band + 1, me), has_up))):
            launch(functools.partial(
                lambda way, device: remote(
                    s.edge_out.at[i, way], s.edge_in.at[i, way],
                    s.sedge.at[i, way], s.redge.at[i, way], device), way, device), has)

    def wait_edges(i):
        for way, has in enumerate((has_up, has_down)):
            await_recv(functools.partial(
                lambda way: remote(
                    s.edge_out.at[i, way], s.edge_in.at[i, way],
                    s.sedge.at[i, way], s.redge.at[i, way], (band + 1 - 2 * way, me)), way), has)

    def column_of(i, way):
        tile8 = s.edge_in[i, way]
        return jnp.concatenate([tile8, jnp.zeros((L - 8, L), f32)], axis=0).T

    def reduce_send(i):
        for d, e in STEPS:
            launch(functools.partial(
                lambda d, e: remote(
                    s.part.at[i], s.red1.at[i, me], s.sa.at[i, d, e], s.ra.at[i, d, e],
                    (band, to_dev(d, e))), d, e))
        s.red1[i, me] = s.part[i]

    def reduce_middle(i):
        for d, e in STEPS:
            origin = from_dev(d, e)
            remote(s.part.at[i], s.red1.at[i, origin], s.sa.at[i, d, e], s.ra.at[i, d, e],
                   (band, origin)).wait_recv()
        value = s.red1[i, 0]
        for place in range(1, G):
            value = value + s.red1[i, place]
        s.middle[i] = value
        s.red2[i, band] = value
        for step in range(1, bands):
            launch(functools.partial(
                lambda step: remote(
                    s.middle.at[i], s.red2.at[i, band], s.sb.at[i, step], s.rb.at[i, step],
                    ((band + step) % bands, me)), step))

    def reduce_end(i):
        for step in range(1, bands):
            origin = (band - step + bands) % bands
            remote(s.middle.at[i], s.red2.at[i, origin], s.sb.at[i, step], s.rb.at[i, step],
                   (origin, me)).wait_recv()
        value = s.red2[i, 0]
        for place in range(1, bands):
            value = value + s.red2[i, place]
        return [jnp.sum(value[k], keepdims=True) for k in range(2)]

    def eights(value):
        return value.reshape(value.shape[0] // 8, 8, L).sum(axis=0)

    def weight_of(at):
        wave = s.wave[at, :]
        edge = (wave == 0.0) | (wave == 4.0)
        return jnp.where(edge, np.float32(1.0 / total), np.float32(2.0 / total))

    send_phase1(0, 1)
    send_phase1(0, 0)

    blocks = R // 128

    def shifted(index, by=8):
        return pl.ds(pl.multiple_of(index * 128 + by, 8), 128)

    for load in loads[4:]:
        load.wait()
    for ref in (s.east_wet, s.north):
        ref[:, length:R, :] = jnp.zeros((2, R - length, L), f32)

    def make_faces(start, count):
        at, at8 = pl.ds(start, count), eight_on(start, count)
        for k in range(2):
            lanes = slice(k * L, (k + 1) * L)
            wet = s.wet[k, at8, :]
            s.east_wet[k, at, :] = s.eastc[at, lanes] * wet
            s.north[k, at, :] = s.northc[at, lanes] * wet

    loop_rows(make_faces)
    west_dev, east_dev = (me + G - 1) % G, (me + 1) % G
    s.row_out[0] = s.wet[:, 8:16, :]
    s.row_out[1] = s.wet[:, 8 + last_tile : 16 + last_tile, :]
    s.row_out[2] = s.east_wet[:, last_tile : last_tile + 8, :]
    for k, device in enumerate((west_dev, east_dev, east_dev)):
        src = s.row_out.at[k]
        launch(functools.partial(
            lambda k, src, device: remote(
                src, s.row_in.at[k], s.srow.at[k, 0], s.rrow.at[k, 0], (band, device)), k, src, device))

    def take_edges(i, low, high, by):
        for b in range(blocks):
            s.edge_out[i, 0, b : b + 1, :] = low[pl.ds(128 * b + by[0], 128), :].T[:1, :]
            s.edge_out[i, 1, b : b + 1, :] = high[pl.ds(128 * b + by[1], 128), :].T[L - 1 :, :]
        if blocks < 8:
            s.edge_out[i, :, blocks:, :] = jnp.zeros((2, 8 - blocks, L), f32)

    take_edges(0, s.wet.at[0], s.north.at[1], (8, 0))
    send_edges(0)
    for way, (device, has) in enumerate((((band - 1, me), has_down), ((band + 1, me), has_up))):
        launch(functools.partial(
            lambda way, device: remote(
                s.zonal, s.zonal_in.at[way], s.szon.at[way], s.rzon.at[way], device), way, device), has)

    def send_stag():
        return remote(s.staggered.at[1], s.carried, s.sstag, s.rstag, (band + 1, me))

    launch(send_stag, has_up)
    for way, has in enumerate((has_up, has_down)):
        @pl.when(jnp.logical_not(has))
        def _(way=way):
            for i in range(2):
                s.edge_in[i, way] = jnp.zeros((8, L), f32)
                s.zgot[i, way] = jnp.zeros((PD, L), f32)
            s.zonal_in[way] = jnp.zeros((1, 2 * L), f32)

    @pl.when(jnp.logical_not(has_down))
    def _():
        s.carried[...] = jnp.zeros((L, L), f32)

    loads[2].wait()
    loads[3].wait()

    def turn(index):
        at = span(index)
        for k in range(2):
            s.turned[k, at, :] = s.matrix[k, :, at].T

    loop(W // 128, turn)

    outer_forward(0, 1)
    outer_forward(0, 0)

    for way, has in enumerate((has_up, has_down)):
        await_recv(functools.partial(
            lambda way: remote(
                s.zonal, s.zonal_in.at[way], s.szon.at[way], s.rzon.at[way],
                (band + 1 - 2 * way, me)), way), has)
    z0, z1 = s.zonal[:, :L], s.zonal[:, L:]
    mask1 = lanes_left(1)
    zone_a, zone_b = jnp.where(mask1, z1, z0), jnp.where(mask1, z0, z1)
    is_low = core == 0
    zones = (
        jnp.where(is_low, zone_a, zone_b),
        jnp.where(is_low, zone_b, zone_a),
        jnp.where(mask1, s.zonal_in[0, :, :L], s.zonal_in[1, :, L:]),
    )

    def make_scale(index):
        at = span(index)
        wave = s.wave[at, :]
        for k, zone in enumerate(zones):
            s.scale[k, at, :] = lax.rsqrt(1.0 + wave * zone)
        s.scale_out[at, :] = s.scale[0, at, :] * weight_of(at)

    loop(W // 128, make_scale)

    @pl.when(has_down)
    def _():
        remote(s.staggered.at[1], s.carried, s.sstag, s.rstag, (band - 1, me)).wait_recv()

    def swapped(value):
        value = jnp.concatenate([value[half:, :], value[:half, :]], axis=0)
        return pltpu.roll(value, half, 1)

    row_top = lax.broadcasted_iota(jnp.int32, (L, L), 0) < half
    col_left = lanes_left(L)
    tl, tr = row_top & col_left, row_top & jnp.logical_not(col_left)
    bl = jnp.logical_not(row_top) & col_left
    br = jnp.logical_not(row_top) & jnp.logical_not(col_left)
    al0, al1 = s.aligned[0], s.aligned[1]
    mid, top, low = swapped(s.staggered[0]), swapped(s.staggered[1]), swapped(s.carried[...])
    zero = jnp.zeros((L, L), f32)

    def pick(*items):
        value = zero
        for where, block in items:
            value = jnp.where(where, block, value)
        return value

    own = jnp.where(
        is_low, mid + pick((tl, al1), (br, al0)), pick((tl, al0 + low), (br, al1 + top)))
    beside = jnp.where(is_low, pick((tr, al0), (bl, al1)), pick((tr, al1), (bl, al0)))
    across = pick((tr, top), (bl, low))
    for k, value in enumerate((own, beside)):
        hi, lo = parted(value)
        s.gain[0, k * L : (k + 1) * L, :] = hi
        s.gain[1, k * L : (k + 1) * L, :] = lo
    hi, lo = parted(across)
    s.gain_z[0] = hi
    s.gain_z[1] = lo

    relay(0)
    own_spectrum(0)
    wait_mate(0)
    mate_spectrum(0)
    mix(0)
    inner_back(0)

    def rz_part(index, carry):
        at = span(index)
        return carry + eights(s.spec[0, at, :] * (s.mixed[0, at, :] * weight_of(at)))

    s.part[0, 0] = lax.fori_loop(0, W // 128, rz_part, jnp.zeros((8, L), f32))

    for k, device in enumerate((east_dev, west_dev, west_dev)):
        remote(s.row_out.at[k], s.row_in.at[k], s.srow.at[k, 0], s.rrow.at[k, 0], (band, device)).wait_recv()
    wait_edges(0)
    north_col, south_col = column_of(0, 0), column_of(0, 1)
    for k in range(2):
        s.wet[k, 8 + length : 9 + length, :] = s.row_in[0, k, 0:1, :]
        s.east[k, 7:8, :] = s.row_in[2, k, last_row : last_row + 1, :] * s.wet[k, 8:9, :]
    lane = lax.broadcasted_iota(jnp.int32, (128, L), 1)
    first_lane, last_lane = lane == 0, lane == L - 1
    for b in range(blocks):
        at, at8, at9 = pl.ds(128 * b, 128), pl.ds(128 * b + 8, 128), pl.ds(128 * b + 9, 128)
        wet = [s.wet[k, at8, :] for k in range(2)]
        east = [s.east_wet[k, at, :] * s.wet[k, at9, :] for k in range(2)]
        moved = [pltpu.roll(value, L - 1, 1) for value in wet]
        beyond = jnp.broadcast_to(north_col[:, b : b + 1], (128, L))
        north = [
            s.north[0, at, :] * jnp.where(last_lane, moved[1], moved[0]),
            s.north[1, at, :] * jnp.where(last_lane, beyond, moved[1]),
        ]
        moved = [pltpu.roll(value, 1, 1) for value in north]
        beyond = jnp.broadcast_to(south_col[:, b : b + 1], (128, L))
        south = [
            jnp.where(first_lane, beyond * wet[0], moved[0]),
            jnp.where(first_lane, moved[0], moved[1]),
        ]
        for k in range(2):
            s.east[k, at8, :] = east[k]
            s.north[k, at, :] = north[k]
            s.south[k, at, :] = south[k]
    def make_diag(start, count):
        at, at8 = pl.ds(start, count), eight_on(start, count)
        for k in range(2):
            wet = s.wet[k, at8, :]
            own = (1.0 - wet) + wet * s.selfc[at, k * L : (k + 1) * L]
            s.diag[k, at, :] = own + s.diag[k, at, :]

    for b in range(blocks):
        at, at8, at7 = pl.ds(128 * b, 128), pl.ds(128 * b + 8, 128), pl.ds(128 * b + 7, 128)
        for k in range(2):
            s.diag[k, at, :] = (
                (s.east[k, at8, :] + s.east[k, at7, :]) + (s.north[k, at, :] + s.south[k, at, :]))
    s.diag[:, length:R, :] = jnp.zeros((2, R - length, L), f32)
    loop_rows(make_diag)
    if R > PD:
        for t in range(2):
            for g in range(2):
                s.got4[t, g, PD:, :] = jnp.zeros((R - PD, L), f32)

    outer_back(0, 0, True)
    outer_back(0, 1, True)
    wait_back(0, 0, True)
    wait_back(0, 1, True)

    def fields_of(t, at, count):
        a, b = s.got4[t, 0, at, :], s.got4[t, 1, at, :]
        mask = lanes_left(count)
        return jnp.where(mask, b, a), jnp.where(mask, a, b)

    def make_field(index):
        at8 = shifted(index)
        for k, value in enumerate(fields_of(0, span(index), 128)):
            s.field[k, at8, :] = s.wet[k, at8, :] * value

    loop(blocks, make_field)
    take_edges(1, s.field.at[0], s.field.at[1], (8, 8))
    send_edges(1)
    mask1 = lanes_left(1)
    for way, (row, source) in enumerate(((0, 0), (last_row, 1))):
        a, b = s.ew[way, 0, row : row + 1, :], s.ew[way, 1, row : row + 1, :]
        for k, value in enumerate((jnp.where(mask1, b, a), jnp.where(mask1, a, b))):
            at = 8 + length if way == 0 else 7
            s.field[k, at : at + 1, :] = s.row_in[source, k, row : row + 1, :] * value

    curvature = jnp.zeros((8, L), f32)
    for b in range(blocks):
        at, at8 = pl.ds(128 * b, 128), pl.ds(128 * b + 8, 128)
        at7, at9 = pl.ds(128 * b + 7, 128), pl.ds(128 * b + 9, 128)
        here = [s.field[k, at8, :] for k in range(2)]
        up = [pltpu.roll(value, L - 1, 1) for value in here]
        down = [pltpu.roll(value, 1, 1) for value in here]
        up = [jnp.where(last_lane, up[1], up[0]), jnp.where(last_lane, 0.0, up[1])]
        down = [jnp.where(first_lane, 0.0, down[0]), jnp.where(first_lane, down[0], down[1])]
        image = []
        for k in range(2):
            value = s.diag[k, at, :] * here[k]
            value = value - s.east[k, at8, :] * s.field[k, at9, :]
            value = value - s.east[k, at7, :] * s.field[k, at7, :]
            value = value - s.north[k, at, :] * up[k]
            value = value - s.south[k, at, :] * down[k]
            if 128 * (b + 1) > length:
                row = lax.broadcasted_iota(jnp.int32, (128, L), 0)
                value = jnp.where(row < length - 128 * b, value, 0.0)
            image.append(value)
            curvature = curvature + eights(here[k] * image[k])
        s.xs[1, 0, at, :], s.xs[1, 1, at, :] = groups_of(*image)

    send_phase1(1, 0)
    wait_edges(1)
    north_col, south_col = column_of(1, 0), column_of(1, 1)
    for b in range(blocks):
        at, at8 = pl.ds(128 * b, 128), pl.ds(128 * b + 8, 128)
        south = s.south[0, at, :] * jnp.broadcast_to(south_col[:, b : b + 1], (128, L))
        north = s.north[1, at, :] * jnp.broadcast_to(north_col[:, b : b + 1], (128, L))
        extra = jnp.where(first_lane, south, jnp.where(last_lane, north, 0.0))
        s.xs[1, 1, at, :] = s.xs[1, 1, at, :] - extra
        here = jnp.where(first_lane, s.field[0, at8, :], s.field[1, at8, :])
        curvature = curvature - eights(here * extra)
    send_phase1(1, 1)
    s.part[0, 1] = curvature
    reduce_send(0)

    outer_forward(1, 0)
    reduce_middle(0)
    outer_forward(1, 1)
    relay(1)
    own_spectrum(1)
    wait_mate(1)
    mate_spectrum(1)
    mix(1)
    inner_back(1)
    rz_now, bend = reduce_end(0)
    alpha = rz_now / bend

    def rz_next_part(index, carry):
        at = span(index)
        spectrum = s.spec[0, at, :] - alpha * s.spec[1, at, :]
        mixed = s.mixed[0, at, :] - alpha * s.mixed[1, at, :]
        return carry + eights(spectrum * (mixed * weight_of(at)))

    s.part[1, 0] = lax.fori_loop(0, W // 128, rz_next_part, jnp.zeros((8, L), f32))
    s.part[1, 1] = jnp.zeros((8, L), f32)
    reduce_send(1)

    outer_back(1, 0, False)
    outer_back(1, 1, False)
    reduce_middle(1)

    def first_outputs(start, count):
        at, at8 = pl.ds(start, count), eight_on(start, count)
        a, b = s.xs[0, 0, at, :], s.xs[0, 1, at, :]
        image_a, image_b = s.xs[1, 0, at, :], s.xs[1, 1, at, :]
        rest_a, rest_b = a - alpha * image_a, b - alpha * image_b
        mask = lanes_left(count)
        s.out[1, at, :L] = jnp.where(mask, rest_b, rest_a)
        s.out[1, at, L:] = jnp.where(mask, rest_a, rest_b)
        for k in range(2):
            s.out[0, at, k * L : (k + 1) * L] = alpha * s.field[k, at8, :]

    loop_rows(first_outputs)
    stores = [
        pltpu.make_async_copy(s.out.at[k], ref, s.store.at[k])
        for k, ref in enumerate((solution_ref, residual_ref, direction_ref))
    ]
    stores[0].start()
    stores[1].start()
    rz_next, _ = reduce_end(1)
    beta = rz_next / rz_now
    wait_back(1, 0, False)
    wait_back(1, 1, False)

    def last_output(start, count):
        at, at8 = pl.ds(start, count), eight_on(start, count)
        for k, value in enumerate(fields_of(1, at, count)):
            first = s.field[k, at8, :]
            second = first - alpha * (s.wet[k, at8, :] * value)
            s.out[2, at, k * L : (k + 1) * L] = second + beta * first

    loop_rows(last_output)
    stores[2].start()
    for make, when in pending:
        if when is None:
            make().wait_send()
        else:
            pl.when(when)(functools.partial(lambda make: make().wait_send(), make))
    for store in stores:
        store.wait()


def local(
    surface_forcing,
    ocean_mask,
    self_coupling,
    east_coupling,
    north_coupling,
    zonal_weight,
    aligned_inverse,
    staggered_inverse,
):
    groups, bands = lax.axis_size("lon"), lax.axis_size("lat")
    length, columns = surface_forcing.shape
    block = aligned_inverse.shape[1]
    assert columns == 2 * block and block == 128 and groups % 4 == 0
    chunk = -(-length // (8 * groups)) * 8
    padded = groups * chunk
    while 2 * padded % 128:
        chunk, padded = chunk + 8, padded + 8 * groups
    plan = Plan(groups, bands, length, columns, block, (chunk, padded))
    assert plan.rows <= 1024
    matrix, waves = inner_tables(groups, length, padded)
    lanes = np.repeat(waves[:, :, None], block, axis=2)
    scratch = plan.scratch()
    anywhere = pl.BlockSpec(memory_space=pl.ANY)
    shape = jax.ShapeDtypeStruct((length, columns), jnp.float32)
    return pl.pallas_call(
        functools.partial(kernel, plan, tuple(scratch)),
        out_shape=(shape, shape, shape),
        in_specs=[anywhere] * 10,
        out_specs=(anywhere,) * 3,
        scratch_shapes=list(scratch.values()),
        compiler_params=pltpu.CompilerParams(
            collective_id=0, has_side_effects=True, vmem_limit_bytes=60 * 2**20
        ),
        name="step",
    )(
        surface_forcing, ocean_mask, self_coupling, east_coupling, north_coupling,
        zonal_weight[None, :], aligned_inverse, staggered_inverse,
        jnp.asarray(matrix), jnp.asarray(lanes),
    )


def solution(mesh):
    grid = P("lon", "lat")
    stack = P("lat", None, None)
    return jax.shard_map(
        local,
        mesh=mesh,
        in_specs=(grid, grid, grid, grid, grid, P("lat"), stack, stack),
        out_specs=(grid, grid, grid),
        check_vma=False,
    )
```

profile of v0, /device:TPU:0, one launch (start us, length us, event | category | flops | bytes accessed | tf_op | source)
XLA Modules:
  0.0 90.6 jit_solution(487345496020199345)
XLA Ops:
  0.6 84.2 %step.1 = (f32[540,256]{1,0:T(8,128)}, f32[540,256]{1,0:T(8,128)}, f32[540,256]{1,0:T(8,128)}) custom-call(f32[540,256]{1,0:T(8,128)} %refs_0_.1, s32[540,256]{1,0:T(8,128)} %refs_1_.1, f32[540,256]{1,0:T(8,128)} %refs_2_.1, f32[540,256]{1,0:T(8,128)} %refs_3_.1, f32[540,256]{1,0:T(8,128)} %refs_4_.1, f32[1,256]{1,0:T(1,128)} %bitcast.1, ...), custom_call_target="tpu_custom_call" | custom-call | tf_op jit(solution)/shard_map/step/pallas_call | solution.py:919
  84.9 1.9 %copy.16 = f32[540,256]{1,0:T(8,128)} copy(f32[540,256]{1,0:T(8,128)} %get-tuple-element.6) | data formatting | bytes 1105920
  86.8 1.9 %copy.17 = f32[540,256]{1,0:T(8,128)} copy(f32[540,256]{1,0:T(8,128)} %get-tuple-element.7) | data formatting | bytes 1105920
  88.7 1.9 %copy.18 = f32[540,256]{1,0:T(8,128)} copy(f32[540,256]{1,0:T(8,128)} %get-tuple-element.8) | data formatting | bytes 1105920
where the time goes:
time: 90.8 us; the launch traced here: 90.6 us
  Pallas kernels  84.2 us (93%)
  local copies, waits for them, and re-layouts  5.68 us (6%)
    pallas_call x1, Pallas kernels, local(): pl.pallas_call(functools.partial(kernel, plan, tuple(scratch)), out_shape...  84.2 us
    unnamed x3, local copies, waits for them, and re-layouts  5.68 us

commit v1 on v0

--- a/solution.py
+++ b/solution.py
@@ -9,6 +9,7 @@
 from jax.sharding import PartitionSpec as P
 
 MESH = pl.DeviceIdType.MESH
+TILE = 1152
 
 
 def outer_table(groups):
@@ -91,7 +92,7 @@
         self.chunk, self.padded = width_of
         self.width = 2 * self.padded
         self.rows = max(-(-length // 128) * 128, -(-self.padded // 128) * 128)
-        self.tile = next(t for t in (384, 256, 128) if self.width % t == 0)
+        self.tile = next(t for t in (TILE, 384, 256, 128) if self.width % t == 0)
         self.table = outer_table(groups)
 
     def scratch(self):
@@ -127,18 +128,14 @@
             "edge_in": vmem((2, 2, 8, L), f32),
             "scale": vmem((3, W, L), f32),
             "scale_out": vmem((W, L), f32),
-            "gain": vmem((2, 2 * L, L), bf16),
-            "gain_z": vmem((2, L, L), bf16),
+            "gain": vmem((3, L, 2 * L), bf16),
             "xs": vmem((2, 2, R, L), f32),
             "got1": vmem((2, 2, G, C, L), f32),
             "send2": vmem((2, NP, 2, 2, C, L), f32),
-            "got2": vmem((2, 2, PD, L), f32),
-            "mate2": vmem((2, 2, PD, L), f32),
+            "cells": vmem((2, 3, 2, PD, L), f32),
             "zs": vmem((2, 2, PD, L), f32),
             "zgot": vmem((2, 2, PD, L), f32),
             "spec": vmem((2, W, L), f32),
-            "spec_mate": vmem((W, L), f32),
-            "spec_z": vmem((W, L), f32),
             "mixed": vmem((2, W, L), f32),
             "send3": vmem((2, 2, PD, L), f32),
             "got3": vmem((2, G, 2, C, L), f32),
@@ -150,34 +147,34 @@
             "middle": vmem((2, 2, 8, L), f32),
             "red2": vmem((2, self.bands, 2, 8, L), f32),
             "out": vmem((3, self.length, 2 * L), f32),
-            "load": dma((16,)),
-            "s1": dma((2, 2, NP, 2)),
-            "r1": dma((2, 2, NP, 2)),
-            "s2": dma((2, 2, NP, 2)),
-            "r2": dma((2, NP, 2)),
-            "sm": dma((2, NP, 2)),
-            "rm": dma((2, NP, 2)),
-            "sz": dma((2, 2, NP, 2)),
-            "rz": dma((2, 2, NP, 2)),
-            "s3": dma((2, NP, 2)),
-            "r3": dma((2, NP, 2)),
-            "s4": dma((2, 2, NP, 2)),
-            "r4": dma((2, 2, NP, 2)),
-            "sw": dma((2, 2, NP, 2)),
-            "rw": dma((2, 2)),
-            "srow": dma((3, 2)),
-            "rrow": dma((3, 2)),
+            "store": dma((3,)),
+            "load": dma((10,)),
+            "s1": dma((2, 2)),
+            "r1": dma((2, 2)),
+            "s2": dma((2,)),
+            "r2": dma((2, NP)),
+            "sm": dma((2,)),
+            "rm": dma((2,)),
+            "sz": dma((2, 2)),
+            "rz": dma((2, 2)),
+            "s3": dma((2,)),
+            "r3": dma((2, 2)),
+            "s4": dma((2, 2)),
+            "r4": dma((2, 2)),
+            "sw": dma((2,)),
+            "rw": dma((2,)),
+            "srow": dma,
+            "rrow": dma,
             "sedge": dma((2, 2)),
             "redge": dma((2, 2)),
             "szon": dma((2,)),
             "rzon": dma((2,)),
             "sstag": dma,
             "rstag": dma,
-            "sa": dma((2, NP, 2)),
-            "ra": dma((2, NP, 2)),
-            "sb": dma((2, self.bands)),
-            "rb": dma((2, self.bands)),
-            "store": dma((3,)),
+            "sa": dma((2,)),
+            "ra": dma((2,)),
+            "sb": dma((2,)),
+            "rb": dma((2,)),
         }
 
 
@@ -203,6 +200,7 @@
     pair, core = me // 2, me % 2
     mate = me + 1 - 2 * core
     has_up, has_down = band < bands - 1, band > 0
+    sends_up, sends_down = (core == 1) & has_up, (core == 1) & has_down
     STEPS = [(d, e) for d in range(1, NP) for e in (0, 1)] + [(0, 1)]
     last_chunk = (length - 1) // C
     last_tile = (length - 1) // 8 * 8
@@ -227,13 +225,24 @@
             make().start()
         else:
             pl.when(when)(lambda: make().start())
-        pending.append((make, when))
-
-    def await_recv(make, when=None):
-        if when is None:
-            make().wait_recv()
-        else:
-            pl.when(when)(lambda: make().wait_recv())
+
+    def recv_all(ref, sem, when=None):
+        def wait():
+            remote(ref, ref, sem, sem, (band, mate)).wait_recv()
+        wait() if when is None else pl.when(when)(wait)
+
+    def sent(ref, sem, when=None):
+        pending.append((ref, sem, when))
+
+    def drain():
+        for ref, sem, when in pending:
+            def wait(ref=ref, sem=sem):
+                remote(ref, ref, sem, sem, (band, mate)).wait_send()
+            wait() if when is None else pl.when(when)(wait)
+        pending.clear()
+
+    def chunks(t, count):
+        return s.got3.at[t, pl.ds(0, count)]
 
     def rows(index):
         return pl.ds(pl.multiple_of(index * C, 8), C)
@@ -277,18 +286,21 @@
         (staggered_ref, s.staggered),
     )):
         loads.append(pltpu.make_async_copy(src, dst, s.load.at[index]))
-        loads[-1].start()
+    loads[0].start()
+    loads[1].start()
 
     barrier = pltpu.get_barrier_semaphore()
     for d, e in STEPS:
         pl.semaphore_signal(barrier, inc=1, device_id=(band, to_dev(d, e)), device_id_type=MESH)
-    for step in range(1, bands):
-        pl.semaphore_signal(
-            barrier, inc=1, device_id=((band + step) % bands, me), device_id_type=MESH
-        )
+    for side, has in ((band + 1, has_up), (band - 1, has_down)):
+        @pl.when(has)
+        def _(side=side):
+            pl.semaphore_signal(barrier, inc=1, device_id=(side, me), device_id_type=MESH)
 
     loads[0].wait()
     loads[1].wait()
+    for load in loads[2:]:
+        load.start()
     s.xs[0, :, length:R, :] = jnp.zeros((2, R - length, L), f32)
     s.wet[:, 8 + length : 16 + R, :] = jnp.zeros((2, R + 8 - length, L), f32)
     s.field[:, 8 + R : 16 + R, :] = jnp.zeros((2, 8, L), f32)
@@ -305,21 +317,18 @@
         s.wet[1, at8, :] = wet[:, L:]
 
     loop_rows(make_rhs)
-    pl.semaphore_wait(barrier, G + bands - 2)
+    pl.semaphore_wait(barrier, G - 1 + has_up.astype(jnp.int32) + has_down.astype(jnp.int32))
 
     def send_phase1(t, g):
         for d, e in STEPS:
-            launch(functools.partial(
-                lambda d, e: remote(
-                    s.xs.at[t, g, rows(to_dev(d, e))], s.got1.at[t, g, me],
-                    s.s1.at[t, g, d, e], s.r1.at[t, g, d, e], (band, to_dev(d, e))), d, e))
+            to = to_dev(d, e)
+            remote(s.xs.at[t, g, rows(to)], s.got1.at[t, g, me],
+                   s.s1.at[t, g], s.r1.at[t, g], (band, to)).start()
+        sent(s.got1.at[t, g, pl.ds(0, G - 1)], s.s1.at[t, g])
         s.got1[t, g, me] = s.xs[t, g, rows(me), :]
 
     def outer_forward(t, g):
-        for d, e in STEPS:
-            origin = from_dev(d, e)
-            remote(s.xs.at[t, g, rows(origin)], s.got1.at[t, g, origin],
-                   s.s1.at[t, g, d, e], s.r1.at[t, g, d, e], (band, origin)).wait_recv()
+        recv_all(s.got1.at[t, g, pl.ds(0, G - 1)], s.r1.at[t, g])
 
         def step(index):
             at = span(index, 8)
@@ -328,112 +337,121 @@
                 s.send2[t, row // 2, g, row % 2, at, :] = weighted(values, table[row])
 
         loop(C // 8, step)
-        e = (g + core) % 2
         for d in list(range(1, NP)) + [0]:
-            target = 2 * ((pair + d) % NP) + g
-            launch(functools.partial(
-                lambda d, target: remote(
-                    s.send2.at[t, (pair + d) % NP, g], s.got2.at[t, :, rows(me), :],
-                    s.s2.at[t, g, d, e], s.r2.at[t, d, e], (band, target)), d, target),
-                None if d else core != g)
+            def make(d=d):
+                to = (pair + d) % NP
+                return remote(
+                    s.send2.at[t, to, g], s.cells.at[t, 0, :, rows(me), :],
+                    s.s2.at[t], s.r2.at[t, d], (band, 2 * to + g))
+            launch(make, None if d else core != g)
 
         @pl.when(core == g)
         def _():
-            s.got2[t, :, rows(me), :] = s.send2[t, pair, g]
-
-    def forward_on(t, d, e):
-        origin = from_dev(d, e)
-        at = rows(origin)
-        launch(functools.partial(
-            lambda at, d, e: remote(
-                s.got2.at[t, :, at, :], s.mate2.at[t, :, at, :],
-                s.sm.at[t, d, e], s.rm.at[t, d, e], (band, mate)), at, d, e))
-
-        @pl.when(core == 1)
-        def _():
-            low, high = s.got2[t, 0, at, :], s.got2[t, 1, at, :]
-            mask = lanes_left(C)
-            s.zs[t, 0, at, :] = jnp.where(mask, low, pltpu.roll(high, half, 1))
-            s.zs[t, 1, at, :] = jnp.where(mask, pltpu.roll(low, half, 1), high)
-
-        launch(functools.partial(
-            lambda at, d, e: remote(
-                s.zs.at[t, 0, at, :], s.zgot.at[t, 0, at, :],
-                s.sz.at[t, 0, d, e], s.rz.at[t, 0, d, e], (band - 1, me)), at, d, e),
-            (core == 1) & has_down)
-        launch(functools.partial(
-            lambda at, d, e: remote(
-                s.zs.at[t, 1, at, :], s.zgot.at[t, 1, at, :],
-                s.sz.at[t, 1, d, e], s.rz.at[t, 1, d, e], (band + 1, me)), at, d, e),
-            (core == 1) & has_up)
-
-    def relay(t):
-        forward_on(t, 0, 0)
-        for d, e in [(0, 1)] + [step for step in STEPS if step[0]]:
-            origin = from_dev(d, e)
-            remote(s.send2.at[t, 0, 0], s.got2.at[t, :, rows(origin), :],
-                   s.s2.at[t, 0, d, e], s.r2.at[t, d, e], (band, origin)).wait_recv()
-            forward_on(t, d, e)
+            s.cells[t, 0, :, rows(me), :] = s.send2[t, pair, g]
+
+    def pair_rows(d):
+        return pl.ds(pl.multiple_of((pair - d + NP) % NP * (2 * C), 16), 2 * C)
+
+    def relay(t, steps):
+        for d in steps:
+            recv_all(chunks(t, 2 if d else 1), s.r2.at[t, d])
+            at = pair_rows(d)
+            remote(s.cells.at[t, 0, :, at, :], s.cells.at[t, 1, :, at, :],
+                   s.sm.at[t], s.rm.at[t], (band, mate)).start()
+
+            @pl.when(core == 1)
+            def _():
+                low, high = s.cells[t, 0, 0, at, :], s.cells[t, 0, 1, at, :]
+                mask = lanes_left(2 * C)
+                s.zs[t, 0, at, :] = jnp.where(mask, low, pltpu.roll(high, half, 1))
+                s.zs[t, 1, at, :] = jnp.where(mask, pltpu.roll(low, half, 1), high)
+
+            for way, has in ((0, sends_down), (1, sends_up)):
+                def make(way=way):
+                    return remote(s.zs.at[t, way, at, :], s.zgot.at[t, way, at, :],
+                                  s.sz.at[t, way], s.rz.at[t, way], (band - 1 + 2 * way, me))
+                launch(make, has)
 
     def wait_mate(t):
-        for d, e in [(0, 0)] + STEPS:
-            at = rows(2 * ((pair - d + NP) % NP) + (1 - core + e) % 2)
-            remote(s.got2.at[t, :, at, :], s.mate2.at[t, :, at, :],
-                   s.sm.at[t, d, e], s.rm.at[t, d, e], (band, mate)).wait_recv()
-
-    def transform(source, scale, put):
-        hi, lo = parted(source)
+        recv_all(s.cells.at[t, 1], s.rm.at[t])
+
+    def wait_across(t):
+        for way, has in ((0, has_up), (1, has_down)):
+            recv_all(s.zgot.at[t, way], s.rz.at[t, way], has)
+
+        def step(index):
+            size = G // 2 * C
+            at = pl.ds(pl.multiple_of(index * size, 8), size)
+            above, below = s.zgot[t, 0, at, :], s.zgot[t, 1, at, :]
+            mask = lanes_left(size)
+            s.cells[t, 2, 0, at, :] = jnp.where(mask, above, pltpu.roll(below, half, 1))
+            s.cells[t, 2, 1, at, :] = jnp.where(mask, pltpu.roll(above, half, 1), below)
+
+        loop(2, step)
+
+    def transform(t, which, start):
+        hi, lo = parted(s.cells[t, which].reshape(W, L))
         both = jnp.concatenate([hi, lo], axis=1)
 
         def step(index):
             at = span(index, tile)
             wide = dot(s.matrix[0, at, :], both)
             value = wide[:, :L] + (wide[:, L:] + dot(s.matrix[1, at, :], hi))
-            put(at, value * scale[at, :])
+            value = value * s.scale[which, at, :]
+
+            @pl.when(which == 0)
+            def _():
+                s.spec[t, at, :] = value
+
+            high, low = parted(value)
+            wide = dot(high, s.gain[which])
+            mixed = wide[:, :L] + (wide[:, L:] + dot(low, s.gain[which, :, :L]))
+            if not start:
+                mixed = mixed + s.mixed[t, at, :]
+            s.mixed[t, at, :] = mixed
 
         loop(W // tile, step)
 
-    def put_in(ref):
-        def put(at, value):
-            ref[at, :] = value
-        return put
-
-    def own_spectrum(t):
-        transform(s.got2[t].reshape(W, L), s.scale.at[0], put_in(s.spec.at[t]))
-
-    def mate_spectrum(t):
-        transform(s.mate2[t].reshape(W, L), s.scale.at[1], put_in(s.spec_mate))
-
-    def mix(t):
-        def step(index):
-            at = span(index, tile)
-            hi, lo = parted(jnp.concatenate([s.spec[t, at, :], s.spec_mate[at, :]], axis=1))
-            s.mixed[t, at, :] = dot(hi, s.gain[0]) + (dot(lo, s.gain[0]) + dot(hi, s.gain[1]))
-
-        loop(W // tile, step)
-
-        @pl.when(core == 1)
+    NEAR, FAR = [0], list(range(1, NP))
+
+    def inner_forward(t, late):
+        early = core != late
+
+        @pl.when(early)
         def _():
-            for d, e in [(0, 0)] + STEPS:
-                for way, has in ((0, has_up), (1, has_down)):
-                    def wait(way=way, d=d, e=e):
-                        at = rows(from_dev(d, e))
-                        remote(s.zs.at[t, way, at, :], s.zgot.at[t, way, at, :],
-                               s.sz.at[t, way, d, e], s.rz.at[t, way, d, e],
-                               (band + 1 - 2 * way, me)).wait_recv()
-                    pl.when(has)(wait)
-            above, below = s.zgot[t, 0], s.zgot[t, 1]
-            mask = lanes_left(PD)
-            cells = jnp.concatenate([
-                jnp.where(mask, above, pltpu.roll(below, half, 1)),
-                jnp.where(mask, pltpu.roll(above, half, 1), below)], axis=0)
-
-            def put(at, value):
-                hi, lo = parted(value)
-                s.mixed[t, at, :] = s.mixed[t, at, :] + (
-                    dot(hi, s.gain_z[0]) + (dot(lo, s.gain_z[0]) + dot(hi, s.gain_z[1])))
-
-            transform(cells, s.scale.at[2], put)
+            relay(t, NEAR + FAR)
+
+        @pl.when(jnp.logical_not(early))
+        def _():
+            relay(t, NEAR)
+            wait_mate(t)
+
+        sent(chunks(t, G - 1), s.s2.at[t])
+        sent(s.cells.at[t, 1], s.sm.at[t])
+        sent(s.zgot.at[t, 0], s.sz.at[t, 0], sends_down)
+        sent(s.zgot.at[t, 1], s.sz.at[t, 1], sends_up)
+        transform(t, jnp.where(early, 0, 1), True)
+
+        @pl.when(jnp.logical_not(early))
+        def _():
+            relay(t, FAR)
+
+        def outer_part():
+            @pl.when(core == 1)
+            def _():
+                wait_across(t)
+                transform(t, 2, False)
+
+        if late == 0:
+            outer_part()
+
+        @pl.when(early)
+        def _():
+            wait_mate(t)
+
+        transform(t, jnp.where(early, 1, 0), False)
+        if late == 1:
+            outer_part()
 
     def inner_back(t):
         hi, lo = parted(s.mixed[t] * s.scale_out[...])
@@ -448,23 +466,17 @@
                 s.send3[t, part, pl.ds(pl.multiple_of(side * size, 8), size), :] = (
                     wide[:, :L] + (wide[:, L:] + dot(s.turned[1, at, :], hi)))
             for d, e in STEPS:
-                to = to_dev(d, e)
-                launch(functools.partial(
-                    lambda d, e, to: remote(
-                        s.send3.at[t, :, rows(to), :], s.got3.at[t, me],
-                        s.s3.at[t, d, e], s.r3.at[t, d, e], (band, to)), d, e, to),
-                    to // (G // 2) == side)
+                def make(d=d, e=e):
+                    to = to_dev(d, e)
+                    return remote(s.send3.at[t, :, rows(to), :], s.got3.at[t, me],
+                                  s.s3.at[t], s.r3.at[t, core], (band, to))
+                launch(make, to_dev(d, e) // (G // 2) == side)
+        sent(chunks(t, G - 1), s.s3.at[t])
         s.got3[t, me] = s.send3[t, :, rows(me), :]
 
     def outer_back(t, g, edges):
-        e = (g + core) % 2
-        for d in range(NP):
-            origin = 2 * ((pair - d + NP) % NP) + g
-            await_recv(functools.partial(
-                lambda d, origin: remote(
-                    s.send3.at[t, :, rows(0), :], s.got3.at[t, origin],
-                    s.s3.at[t, d, e], s.r3.at[t, d, e], (band, origin)), d, origin),
-                None if d else core != g)
+        recv_all(chunks(t, NP), s.r3.at[t, g], core != g)
+        recv_all(chunks(t, NP - 1), s.r3.at[t, g], core == g)
 
         def step(index):
             at = span(index, 8)
@@ -474,51 +486,44 @@
 
         loop(C // 8, step)
         for d, e in STEPS:
-            launch(functools.partial(
-                lambda d, e: remote(
-                    s.send4.at[t, to_dev(d, e), g], s.got4.at[t, g, rows(me), :],
-                    s.s4.at[t, g, d, e], s.r4.at[t, g, d, e], (band, to_dev(d, e))), d, e))
+            to = to_dev(d, e)
+            remote(s.send4.at[t, to, g], s.got4.at[t, g, rows(me), :],
+                   s.s4.at[t, g], s.r4.at[t, g], (band, to)).start()
+        sent(s.got1.at[t, g, pl.ds(0, G - 1)], s.s4.at[t, g])
         s.got4[t, g, rows(me), :] = s.send4[t, me, g]
         if not edges:
             return
         for way, (owner, shift, at) in enumerate((
             (0, 1, 0), (last_chunk, G - 1, (length - 1) % C // 8 * 8))):
-            for d, e in STEPS:
-                launch(functools.partial(
-                    lambda way, shift, at, d, e: remote(
-                        s.send4.at[t, (to_dev(d, e) + shift) % G, g, pl.ds(at, 8), :], s.ew.at[way, g],
-                        s.sw.at[way, g, d, e], s.rw.at[way, g], (band, to_dev(d, e))),
-                    way, shift, at, d, e), me == owner)
-
             @pl.when(me == owner)
             def _(way=way, shift=shift, at=at):
+                for d, e in STEPS:
+                    to = to_dev(d, e)
+                    remote(s.send4.at[t, (to + shift) % G, g, pl.ds(at, 8), :], s.ew.at[way, g],
+                           s.sw.at[way], s.rw.at[way], (band, to)).start()
                 s.ew[way, g] = s.send4[t, (me + shift) % G, g, pl.ds(at, 8), :]
 
-    def wait_back(t, g, edges):
-        for d, e in STEPS:
-            origin = from_dev(d, e)
-            remote(s.send4.at[t, 0, g], s.got4.at[t, g, rows(origin), :],
-                   s.s4.at[t, g, d, e], s.r4.at[t, g, d, e], (band, origin)).wait_recv()
-        if edges:
-            for way, owner in enumerate((0, last_chunk)):
-                await_recv(functools.partial(
-                    lambda way: remote(
-                        s.send4.at[t, 0, g, pl.ds(0, 8), :], s.ew.at[way, g],
-                        s.sw.at[way, g, 0, 1], s.rw.at[way, g], (band, mate)), way), me != owner)
+            if g == 1:
+                sent(s.red1.at[0, pl.ds(0, G - 1)], s.sw.at[way], me == owner)
+
+    def wait_back(t, g):
+        recv_all(s.got1.at[t, g, pl.ds(0, G - 1)], s.r4.at[t, g])
+
+    def wait_rows():
+        for way, owner in enumerate((0, last_chunk)):
+            recv_all(s.ew.at[way], s.rw.at[way], me != owner)
 
     def send_edges(i):
-        for way, (device, has) in enumerate((((band - 1, me), has_down), ((band + 1, me), has_up))):
-            launch(functools.partial(
-                lambda way, device: remote(
-                    s.edge_out.at[i, way], s.edge_in.at[i, way],
-                    s.sedge.at[i, way], s.redge.at[i, way], device), way, device), has)
+        for way, (side, has) in enumerate(((band - 1, has_down), (band + 1, has_up))):
+            def make(way=way, side=side):
+                return remote(s.edge_out.at[i, way], s.edge_in.at[i, way],
+                              s.sedge.at[i, way], s.redge.at[i, way], (side, me))
+            launch(make, has)
+            sent(s.edge_out.at[i, way], s.sedge.at[i, way], has)
 
     def wait_edges(i):
         for way, has in enumerate((has_up, has_down)):
-            await_recv(functools.partial(
-                lambda way: remote(
-                    s.edge_out.at[i, way], s.edge_in.at[i, way],
-                    s.sedge.at[i, way], s.redge.at[i, way], (band + 1 - 2 * way, me)), way), has)
+            recv_all(s.edge_in.at[i, way], s.redge.at[i, way], has)
 
     def column_of(i, way):
         tile8 = s.edge_in[i, way]
@@ -526,33 +531,25 @@
 
     def reduce_send(i):
         for d, e in STEPS:
-            launch(functools.partial(
-                lambda d, e: remote(
-                    s.part.at[i], s.red1.at[i, me], s.sa.at[i, d, e], s.ra.at[i, d, e],
-                    (band, to_dev(d, e))), d, e))
+            remote(s.part.at[i], s.red1.at[i, me], s.sa.at[i], s.ra.at[i],
+                   (band, to_dev(d, e))).start()
+        sent(s.red1.at[i, pl.ds(0, G - 1)], s.sa.at[i])
         s.red1[i, me] = s.part[i]
 
     def reduce_middle(i):
-        for d, e in STEPS:
-            origin = from_dev(d, e)
-            remote(s.part.at[i], s.red1.at[i, origin], s.sa.at[i, d, e], s.ra.at[i, d, e],
-                   (band, origin)).wait_recv()
+        recv_all(s.red1.at[i, pl.ds(0, G - 1)], s.ra.at[i])
         value = s.red1[i, 0]
         for place in range(1, G):
             value = value + s.red1[i, place]
         s.middle[i] = value
         s.red2[i, band] = value
         for step in range(1, bands):
-            launch(functools.partial(
-                lambda step: remote(
-                    s.middle.at[i], s.red2.at[i, band], s.sb.at[i, step], s.rb.at[i, step],
-                    ((band + step) % bands, me)), step))
+            remote(s.middle.at[i], s.red2.at[i, band], s.sb.at[i], s.rb.at[i],
+                   ((band + step) % bands, me)).start()
+        sent(s.red2.at[i, pl.ds(0, bands - 1)], s.sb.at[i])
 
     def reduce_end(i):
-        for step in range(1, bands):
-            origin = (band - step + bands) % bands
-            remote(s.middle.at[i], s.red2.at[i, origin], s.sb.at[i, step], s.rb.at[i, step],
-                   (origin, me)).wait_recv()
+        recv_all(s.red2.at[i, pl.ds(0, bands - 1)], s.rb.at[i])
         value = s.red2[i, 0]
         for place in range(1, bands):
             value = value + s.red2[i, place]
@@ -593,10 +590,8 @@
     s.row_out[1] = s.wet[:, 8 + last_tile : 16 + last_tile, :]
     s.row_out[2] = s.east_wet[:, last_tile : last_tile + 8, :]
     for k, device in enumerate((west_dev, east_dev, east_dev)):
-        src = s.row_out.at[k]
-        launch(functools.partial(
-            lambda k, src, device: remote(
-                src, s.row_in.at[k], s.srow.at[k, 0], s.rrow.at[k, 0], (band, device)), k, src, device))
+        remote(s.row_out.at[k], s.row_in.at[k], s.srow, s.rrow, (band, device)).start()
+    sent(s.row_in, s.srow)
 
     def take_edges(i, low, high, by):
         for b in range(blocks):
@@ -607,15 +602,18 @@
 
     take_edges(0, s.wet.at[0], s.north.at[1], (8, 0))
     send_edges(0)
-    for way, (device, has) in enumerate((((band - 1, me), has_down), ((band + 1, me), has_up))):
-        launch(functools.partial(
-            lambda way, device: remote(
-                s.zonal, s.zonal_in.at[way], s.szon.at[way], s.rzon.at[way], device), way, device), has)
+    for way, (side, has) in enumerate(((band - 1, has_down), (band + 1, has_up))):
+        def send_zonal(way=way, side=side):
+            return remote(
+                s.zonal, s.zonal_in.at[way], s.szon.at[way], s.rzon.at[way], (side, me))
+        launch(send_zonal, has)
+        sent(s.zonal, s.szon.at[way], has)
 
     def send_stag():
         return remote(s.staggered.at[1], s.carried, s.sstag, s.rstag, (band + 1, me))
 
     launch(send_stag, has_up)
+    sent(s.carried, s.sstag, has_up)
     for way, has in enumerate((has_up, has_down)):
         @pl.when(jnp.logical_not(has))
         def _(way=way):
@@ -642,10 +640,7 @@
     outer_forward(0, 0)
 
     for way, has in enumerate((has_up, has_down)):
-        await_recv(functools.partial(
-            lambda way: remote(
-                s.zonal, s.zonal_in.at[way], s.szon.at[way], s.rzon.at[way],
-                (band + 1 - 2 * way, me)), way), has)
+        recv_all(s.zonal_in.at[way], s.rzon.at[way], has)
     z0, z1 = s.zonal[:, :L], s.zonal[:, L:]
     mask1 = lanes_left(1)
     zone_a, zone_b = jnp.where(mask1, z1, z0), jnp.where(mask1, z0, z1)
@@ -665,9 +660,7 @@
 
     loop(W // 128, make_scale)
 
-    @pl.when(has_down)
-    def _():
-        remote(s.staggered.at[1], s.carried, s.sstag, s.rstag, (band - 1, me)).wait_recv()
+    recv_all(s.carried, s.rstag, has_down)
 
     def swapped(value):
         value = jnp.concatenate([value[half:, :], value[:half, :]], axis=0)
@@ -692,19 +685,12 @@
         is_low, mid + pick((tl, al1), (br, al0)), pick((tl, al0 + low), (br, al1 + top)))
     beside = jnp.where(is_low, pick((tr, al0), (bl, al1)), pick((tr, al1), (bl, al0)))
     across = pick((tr, top), (bl, low))
-    for k, value in enumerate((own, beside)):
+    for k, value in enumerate((own, beside, across)):
         hi, lo = parted(value)
-        s.gain[0, k * L : (k + 1) * L, :] = hi
-        s.gain[1, k * L : (k + 1) * L, :] = lo
-    hi, lo = parted(across)
-    s.gain_z[0] = hi
-    s.gain_z[1] = lo
-
-    relay(0)
-    own_spectrum(0)
-    wait_mate(0)
-    mate_spectrum(0)
-    mix(0)
+        s.gain[k, :, :L] = hi
+        s.gain[k, :, L:] = lo
+
+    inner_forward(0, 0)
     inner_back(0)
 
     def rz_part(index, carry):
@@ -713,8 +699,7 @@
 
     s.part[0, 0] = lax.fori_loop(0, W // 128, rz_part, jnp.zeros((8, L), f32))
 
-    for k, device in enumerate((east_dev, west_dev, west_dev)):
-        remote(s.row_out.at[k], s.row_in.at[k], s.srow.at[k, 0], s.rrow.at[k, 0], (band, device)).wait_recv()
+    recv_all(s.row_in, s.rrow)
     wait_edges(0)
     north_col, south_col = column_of(0, 0), column_of(0, 1)
     for k in range(2):
@@ -761,10 +746,12 @@
             for g in range(2):
                 s.got4[t, g, PD:, :] = jnp.zeros((R - PD, L), f32)
 
+    drain()
     outer_back(0, 0, True)
     outer_back(0, 1, True)
-    wait_back(0, 0, True)
-    wait_back(0, 1, True)
+    wait_back(0, 0)
+    wait_back(0, 1)
+    wait_rows()
 
     def fields_of(t, at, count):
         a, b = s.got4[t, 0, at, :], s.got4[t, 1, at, :]
@@ -823,15 +810,12 @@
     send_phase1(1, 1)
     s.part[0, 1] = curvature
     reduce_send(0)
+    drain()
 
     outer_forward(1, 0)
+    outer_forward(1, 1)
     reduce_middle(0)
-    outer_forward(1, 1)
-    relay(1)
-    own_spectrum(1)
-    wait_mate(1)
-    mate_spectrum(1)
-    mix(1)
+    inner_forward(1, 1)
     inner_back(1)
     rz_now, bend = reduce_end(0)
     alpha = rz_now / bend
@@ -846,18 +830,17 @@
     s.part[1, 1] = jnp.zeros((8, L), f32)
     reduce_send(1)
 
+    drain()
     outer_back(1, 0, False)
+    reduce_middle(1)
     outer_back(1, 1, False)
-    reduce_middle(1)
 
     def first_outputs(start, count):
         at, at8 = pl.ds(start, count), eight_on(start, count)
-        a, b = s.xs[0, 0, at, :], s.xs[0, 1, at, :]
-        image_a, image_b = s.xs[1, 0, at, :], s.xs[1, 1, at, :]
-        rest_a, rest_b = a - alpha * image_a, b - alpha * image_b
         mask = lanes_left(count)
-        s.out[1, at, :L] = jnp.where(mask, rest_b, rest_a)
-        s.out[1, at, L:] = jnp.where(mask, rest_a, rest_b)
+        rest = [s.xs[0, g, at, :] - alpha * s.xs[1, g, at, :] for g in range(2)]
+        s.out[1, at, :L] = jnp.where(mask, rest[1], rest[0])
+        s.out[1, at, L:] = jnp.where(mask, rest[0], rest[1])
         for k in range(2):
             s.out[0, at, k * L : (k + 1) * L] = alpha * s.field[k, at8, :]
 
@@ -870,8 +853,9 @@
     stores[1].start()
     rz_next, _ = reduce_end(1)
     beta = rz_next / rz_now
-    wait_back(1, 0, False)
-    wait_back(1, 1, False)
+    wait_back(1, 0)
+    drain()
+    wait_back(1, 1)
 
     def last_output(start, count):
         at, at8 = pl.ds(start, count), eight_on(start, count)
@@ -882,13 +866,22 @@
 
     loop_rows(last_output)
     stores[2].start()
-    for make, when in pending:
-        if when is None:
-            make().wait_send()
-        else:
-            pl.when(when)(functools.partial(lambda make: make().wait_send(), make))
     for store in stores:
         store.wait()
+    drain()
+
+
+def finish_kernel(*refs):
+    ins, outs, held, arrived, left = refs[:3], refs[3:6], refs[6], refs[7], refs[8]
+    gets = [pltpu.make_async_copy(ref, held.at[k], arrived.at[k]) for k, ref in enumerate(ins)]
+    puts = [pltpu.make_async_copy(held.at[k], ref, left.at[k]) for k, ref in enumerate(outs)]
+    for get in gets:
+        get.start()
+    for get, put in zip(gets, puts):
+        get.wait()
+        put.start()
+    for put in puts:
+        put.wait()
 
 
 def local(
@@ -916,14 +909,14 @@
     scratch = plan.scratch()
     anywhere = pl.BlockSpec(memory_space=pl.ANY)
     shape = jax.ShapeDtypeStruct((length, columns), jnp.float32)
-    return pl.pallas_call(
+    outs = pl.pallas_call(
         functools.partial(kernel, plan, tuple(scratch)),
-        out_shape=(shape, shape, shape),
+        out_shape=(shape,) * 3,
         in_specs=[anywhere] * 10,
         out_specs=(anywhere,) * 3,
         scratch_shapes=list(scratch.values()),
         compiler_params=pltpu.CompilerParams(
-            collective_id=0, has_side_effects=True, vmem_limit_bytes=60 * 2**20
+            collective_id=0, has_side_effects=True, vmem_limit_bytes=61 * 2**20
         ),
         name="step",
     )(
@@ -931,6 +924,18 @@
         zonal_weight[None, :], aligned_inverse, staggered_inverse,
         jnp.asarray(matrix), jnp.asarray(lanes),
     )
+    return pl.pallas_call(
+        finish_kernel,
+        out_shape=(shape,) * 3,
+        in_specs=[anywhere] * 3,
+        out_specs=(anywhere,) * 3,
+        scratch_shapes=[
+            pltpu.VMEM((3, length, columns), jnp.float32),
+            pltpu.SemaphoreType.DMA((3,)),
+            pltpu.SemaphoreType.DMA((3,)),
+        ],
+        name="finish",
+    )(*outs)
 
 
 def solution(mesh):

time: 90.8 us -> 81.6 us (0.90)
  local copies, waits for them, and re-layouts: 5.68 us -> 0 us
  Pallas kernels: 84.2 us -> 80.6 us
    pallas_call x1, Pallas kernels: 84.2 us -> 78.3 us  [local(): pl.pallas_call(functools.partial(kernel, plan, tuple(scratch)), out_shape...]
    unnamed x3 -> x0, local copies, waits for them, and re-layouts: 5.68 us -> none
    pallas_call x0 -> x1, Pallas kernels: none -> 2.28 us  [local(): pl.pallas_call(finish_kernel, out_shape=(shape,) * 3, in_specs=[anywhere]...]
where the time goes in v1:
time: 81.6 us; the launch traced here: 81.4 us
  Pallas kernels  80.6 us (99%)
    pallas_call x1, Pallas kernels, local(): pl.pallas_call(functools.partial(kernel, plan, tuple(scratch)), out_shape...  78.3 us
    pallas_call x1, Pallas kernels, local(): pl.pallas_call(finish_kernel, out_shape=(shape,) * 3, in_specs=[anywhere]...  2.28 us

profile of v1, /device:TPU:0, one launch (start us, length us, event | category | flops | bytes accessed | tf_op | source)
XLA Modules:
  0.0 81.4 jit_solution(4396911898891550657)
XLA Ops:
  0.6 78.3 %step.1 = (f32[540,256]{1,0:T(8,128)}, f32[540,256]{1,0:T(8,128)}, f32[540,256]{1,0:T(8,128)}) custom-call(f32[540,256]{1,0:T(8,128)} %refs_0_.1, s32[540,256]{1,0:T(8,128)} %refs_1_.1, f32[540,256]{1,0:T(8,128)} %refs_2_.1, f32[540,256]{1,0:T(8,128)} %refs_3_.1, f32[540,256]{1,0:T(8,128)} %refs_4_.1, f32[1,256]{1,0:T(1,128)} %bitcast.1, ...), custom_call_target="tpu_custom_call" | custom-call | tf_op jit(solution)/shard_map/step/pallas_call | solution.py:912
  79.0 2.3 %finish.1 = (f32[540,256]{1,0:T(8,128)}, f32[540,256]{1,0:T(8,128)}, f32[540,256]{1,0:T(8,128)}) custom-call(f32[540,256]{1,0:T(8,128)} %get-tuple-element.6.refs_0_, f32[540,256]{1,0:T(8,128)} %get-tuple-element.7.refs_1_, f32[540,256]{1,0:T(8,128)} %get-tuple-element.8.refs_2_), custom_call_target="tpu_custom_call" | custom-call | tf_op jit(solution)/shard_map/finish/pallas_call | solution.py:927

commit v2 on v1

--- a/solution.py
+++ b/solution.py
@@ -9,7 +9,7 @@
 from jax.sharding import PartitionSpec as P
 
 MESH = pl.DeviceIdType.MESH
-TILE = 1152
+TILE = 576
 
 
 def outer_table(groups):
@@ -94,6 +94,14 @@
         self.rows = max(-(-length // 128) * 128, -(-self.padded // 128) * 128)
         self.tile = next(t for t in (TILE, 384, 256, 128) if self.width % t == 0)
         self.table = outer_table(groups)
+        tiles = -(-(-(-length // 8)) // self.pairs)
+        self.pair_size = 8 * tiles
+        self.sizes = (-(-tiles // 2) * 8, tiles // 2 * 8)
+        assert self.sizes[0] <= self.chunk and self.sizes[1] > 0
+        self.pieces = []
+        for size in self.sizes:
+            cut = -(-size // 16) * 8
+            self.pieces.append([(0, cut)] + ([(cut, size - cut)] if cut < size else []))
 
     def scratch(self):
         f32, bf16 = jnp.float32, jnp.bfloat16
@@ -126,16 +134,17 @@
             "row_out": vmem((3, 2, 8, L), f32),
             "edge_out": vmem((2, 2, 8, L), f32),
             "edge_in": vmem((2, 2, 8, L), f32),
-            "scale": vmem((3, W, L), f32),
+            "scale": vmem((2, W, L), f32),
             "scale_out": vmem((W, L), f32),
-            "gain": vmem((3, L, 2 * L), bf16),
+            "gain": vmem((3 * L, 2 * L), bf16),
             "xs": vmem((2, 2, R, L), f32),
             "got1": vmem((2, 2, G, C, L), f32),
             "send2": vmem((2, NP, 2, 2, C, L), f32),
-            "cells": vmem((2, 3, 2, PD, L), f32),
+            "cells": vmem((2, 2, 2, PD, L), f32),
             "zs": vmem((2, 2, PD, L), f32),
             "zgot": vmem((2, 2, PD, L), f32),
             "spec": vmem((2, W, L), f32),
+            "spec_mate": vmem((2, W, L), f32),
             "mixed": vmem((2, W, L), f32),
             "send3": vmem((2, 2, PD, L), f32),
             "got3": vmem((2, G, 2, C, L), f32),
@@ -150,7 +159,7 @@
             "store": dma((3,)),
             "load": dma((10,)),
             "s1": dma((2, 2)),
-            "r1": dma((2, 2)),
+            "r1": dma((2, 2, 2)),
             "s2": dma((2,)),
             "r2": dma((2, NP)),
             "sm": dma((2,)),
@@ -158,7 +167,7 @@
             "sz": dma((2, 2)),
             "rz": dma((2, 2)),
             "s3": dma((2,)),
-            "r3": dma((2, 2)),
+            "r3": dma((2, 2, 2)),
             "s4": dma((2, 2)),
             "r4": dma((2, 2)),
             "sw": dma((2,)),
@@ -202,7 +211,13 @@
     has_up, has_down = band < bands - 1, band > 0
     sends_up, sends_down = (core == 1) & has_up, (core == 1) & has_down
     STEPS = [(d, e) for d in range(1, NP) for e in (0, 1)] + [(0, 1)]
-    last_chunk = (length - 1) // C
+    CP, sizes = plan.pair_size, plan.sizes
+    used = NP * CP
+    last_pair, last_at = (length - 1) // CP, (length - 1) % CP
+    last_core = 1 if last_at >= sizes[0] else 0
+    last_chunk = 2 * last_pair + last_core
+    last_at = (last_at - sizes[0] * last_core) // 8 * 8
+    pieces = ([[(0, size)] for size in sizes], plan.pieces)
     last_tile = (length - 1) // 8 * 8
     last_row = (length - 1) % 8
 
@@ -234,18 +249,31 @@
     def sent(ref, sem, when=None):
         pending.append((ref, sem, when))
 
-    def drain():
-        for ref, sem, when in pending:
+    def drain(keep=0):
+        done = len(pending) - keep
+        for ref, sem, when in pending[:done]:
             def wait(ref=ref, sem=sem):
                 remote(ref, ref, sem, sem, (band, mate)).wait_send()
             wait() if when is None else pl.when(when)(wait)
-        pending.clear()
+        del pending[:done]
 
     def chunks(t, count):
         return s.got3.at[t, pl.ds(0, count)]
 
-    def rows(index):
-        return pl.ds(pl.multiple_of(index * C, 8), C)
+    def row_of(index):
+        return index // 2 * CP + index % 2 * sizes[0]
+
+    def piece_rows(index, start, count):
+        return pl.ds(pl.multiple_of(row_of(index) + start, 8), count)
+
+    def own_of(ref_of, sem, move):
+        for c in range(2):
+            sent(ref_of(sizes[c]), sem, core == c)
+            pl.when(core == c)(functools.partial(move, sizes[c]))
+
+    def for_core(body):
+        for c in range(2):
+            pl.when(core == c)(functools.partial(body, c))
 
     def span(index, size=128):
         return pl.ds(pl.multiple_of(index * size, size), size)
@@ -320,49 +348,67 @@
     pl.semaphore_wait(barrier, G - 1 + has_up.astype(jnp.int32) + has_down.astype(jnp.int32))
 
     def send_phase1(t, g):
-        for d, e in STEPS:
-            to = to_dev(d, e)
-            remote(s.xs.at[t, g, rows(to)], s.got1.at[t, g, me],
-                   s.s1.at[t, g], s.r1.at[t, g], (band, to)).start()
-        sent(s.got1.at[t, g, pl.ds(0, G - 1)], s.s1.at[t, g])
-        s.got1[t, g, me] = s.xs[t, g, rows(me), :]
+        for h in range(len(pieces[t][0])):
+            for d in list(range(1, NP)) + [0]:
+                for c in range(2):
+                    start, count = pieces[t][c][h]
+
+                    def make(d=d, c=c, start=start, count=count):
+                        to = 2 * ((pair + d) % NP) + c
+                        return remote(s.xs.at[t, g, piece_rows(to, start, count)],
+                                      s.got1.at[t, g, me, pl.ds(start, count)],
+                                      s.s1.at[t, g], s.r1.at[t, g, h], (band, to))
+                    launch(make, None if d else core != c)
+
+        def move(size):
+            s.got1[t, g, me, :size, :] = s.xs[t, g, piece_rows(me, 0, size), :]
+
+        own_of(lambda size: s.xs.at[t, g, pl.ds(0, used - size)], s.s1.at[t, g], move)
 
     def outer_forward(t, g):
-        recv_all(s.got1.at[t, g, pl.ds(0, G - 1)], s.r1.at[t, g])
-
-        def step(index):
-            at = span(index, 8)
-            values = [s.got1[t, g, place, at, :] for place in range(G)]
-            for row in range(G):
-                s.send2[t, row // 2, g, row % 2, at, :] = weighted(values, table[row])
-
-        loop(C // 8, step)
-        for d in list(range(1, NP)) + [0]:
-            def make(d=d):
-                to = (pair + d) % NP
-                return remote(
-                    s.send2.at[t, to, g], s.cells.at[t, 0, :, rows(me), :],
-                    s.s2.at[t], s.r2.at[t, d], (band, 2 * to + g))
-            launch(make, None if d else core != g)
+        for h in range(len(pieces[t][0])):
+            for c in range(2):
+                count = pieces[t][c][h][1]
+                recv_all(s.got1.at[t, g, pl.ds(0, G - 1), pl.ds(0, count)], s.r1.at[t, g, h],
+                         core == c)
+
+            def work(c):
+                start, count = pieces[t][c][h]
+
+                def step(index):
+                    at = pl.ds(pl.multiple_of(index * 8 + start, 8), 8)
+                    values = [s.got1[t, g, place, at, :] for place in range(G)]
+                    for row in range(G):
+                        s.send2[t, row // 2, g, row % 2, at, :] = weighted(values, table[row])
+
+                loop(count // 8, step)
+                for d in list(range(1, NP)) + ([] if c == g else [0]):
+                    to = (pair + d) % NP
+                    remote(s.send2.at[t, to, g, :, pl.ds(start, count), :],
+                           s.cells.at[t, 0, :, piece_rows(me, start, count), :],
+                           s.s2.at[t], s.r2.at[t, d], (band, 2 * to + g)).start()
+
+            for_core(work)
 
         @pl.when(core == g)
         def _():
-            s.cells[t, 0, :, rows(me), :] = s.send2[t, pair, g]
+            s.cells[t, 0, :, piece_rows(me, 0, sizes[g]), :] = s.send2[t, pair, g, :, : sizes[g], :]
 
     def pair_rows(d):
-        return pl.ds(pl.multiple_of((pair - d + NP) % NP * (2 * C), 16), 2 * C)
-
-    def relay(t, steps):
-        for d in steps:
-            recv_all(chunks(t, 2 if d else 1), s.r2.at[t, d])
+        return pl.ds(pl.multiple_of((pair - d + NP) % NP * CP, 8), CP)
+
+    def relay(t):
+        for d in range(NP):
+            if d:
+                recv_all(s.send3.at[t, :, pl.ds(0, CP)], s.r2.at[t, d])
+            else:
+                for c in range(2):
+                    recv_all(s.send3.at[t, :, pl.ds(0, sizes[1 - c])], s.r2.at[t, d], core == c)
             at = pair_rows(d)
-            remote(s.cells.at[t, 0, :, at, :], s.cells.at[t, 1, :, at, :],
-                   s.sm.at[t], s.rm.at[t], (band, mate)).start()
-
             @pl.when(core == 1)
             def _():
                 low, high = s.cells[t, 0, 0, at, :], s.cells[t, 0, 1, at, :]
-                mask = lanes_left(2 * C)
+                mask = lanes_left(CP)
                 s.zs[t, 0, at, :] = jnp.where(mask, low, pltpu.roll(high, half, 1))
                 s.zs[t, 1, at, :] = jnp.where(mask, pltpu.roll(low, half, 1), high)
 
@@ -373,90 +419,65 @@
                 launch(make, has)
 
     def wait_mate(t):
-        recv_all(s.cells.at[t, 1], s.rm.at[t])
+        recv_all(s.spec_mate.at[t], s.rm.at[t])
 
     def wait_across(t):
         for way, has in ((0, has_up), (1, has_down)):
-            recv_all(s.zgot.at[t, way], s.rz.at[t, way], has)
+            recv_all(s.zgot.at[t, way, pl.ds(0, used)], s.rz.at[t, way], has)
 
         def step(index):
             size = G // 2 * C
             at = pl.ds(pl.multiple_of(index * size, 8), size)
             above, below = s.zgot[t, 0, at, :], s.zgot[t, 1, at, :]
             mask = lanes_left(size)
-            s.cells[t, 2, 0, at, :] = jnp.where(mask, above, pltpu.roll(below, half, 1))
-            s.cells[t, 2, 1, at, :] = jnp.where(mask, pltpu.roll(above, half, 1), below)
+            s.cells[t, 1, 0, at, :] = jnp.where(mask, above, pltpu.roll(below, half, 1))
+            s.cells[t, 1, 1, at, :] = jnp.where(mask, pltpu.roll(above, half, 1), below)
 
         loop(2, step)
 
-    def transform(t, which, start):
+    def mix_in(t, at, value, which, start):
+        gain = s.gain[which * L : (which + 1) * L, :]
+        high, low = parted(value)
+        wide = dot(high, gain)
+        mixed = wide[:, :L] + (wide[:, L:] + dot(low, gain[:, :L]))
+        s.mixed[t, at, :] = mixed if start else mixed + s.mixed[t, at, :]
+
+    def transform(t, which):
         hi, lo = parted(s.cells[t, which].reshape(W, L))
         both = jnp.concatenate([hi, lo], axis=1)
-
-        def step(index):
-            at = span(index, tile)
+        for start in range(0, W, tile):
+            at = pl.ds(start, tile)
             wide = dot(s.matrix[0, at, :], both)
             value = wide[:, :L] + (wide[:, L:] + dot(s.matrix[1, at, :], hi))
             value = value * s.scale[which, at, :]
-
-            @pl.when(which == 0)
-            def _():
+            if which == 0:
                 s.spec[t, at, :] = value
-
-            high, low = parted(value)
-            wide = dot(high, s.gain[which])
-            mixed = wide[:, :L] + (wide[:, L:] + dot(low, s.gain[which, :, :L]))
-            if not start:
-                mixed = mixed + s.mixed[t, at, :]
-            s.mixed[t, at, :] = mixed
-
-        loop(W // tile, step)
-
-    NEAR, FAR = [0], list(range(1, NP))
-
-    def inner_forward(t, late):
-        early = core != late
-
-        @pl.when(early)
+                remote(s.spec.at[t, at], s.spec_mate.at[t, at],
+                       s.sm.at[t], s.rm.at[t], (band, mate)).start()
+            mix_in(t, at, value, which, which == 0)
+
+    def inner_forward(t):
+        relay(t)
+        for c in range(2):
+            sent(s.got3.at[t, pl.ds(0, G - 1), :, pl.ds(0, sizes[c])], s.s2.at[t], core == c)
+        sent(s.zgot.at[t, 0, pl.ds(0, used)], s.sz.at[t, 0], sends_down)
+        sent(s.zgot.at[t, 1, pl.ds(0, used)], s.sz.at[t, 1], sends_up)
+        transform(t, 0)
+        sent(s.spec_mate.at[t], s.sm.at[t])
+
+        @pl.when(core == 1)
         def _():
-            relay(t, NEAR + FAR)
-
-        @pl.when(jnp.logical_not(early))
-        def _():
-            relay(t, NEAR)
-            wait_mate(t)
-
-        sent(chunks(t, G - 1), s.s2.at[t])
-        sent(s.cells.at[t, 1], s.sm.at[t])
-        sent(s.zgot.at[t, 0], s.sz.at[t, 0], sends_down)
-        sent(s.zgot.at[t, 1], s.sz.at[t, 1], sends_up)
-        transform(t, jnp.where(early, 0, 1), True)
-
-        @pl.when(jnp.logical_not(early))
-        def _():
-            relay(t, FAR)
-
-        def outer_part():
-            @pl.when(core == 1)
-            def _():
-                wait_across(t)
-                transform(t, 2, False)
-
-        if late == 0:
-            outer_part()
-
-        @pl.when(early)
-        def _():
-            wait_mate(t)
-
-        transform(t, jnp.where(early, 1, 0), False)
-        if late == 1:
-            outer_part()
+            wait_across(t)
+            transform(t, 1)
+
+        wait_mate(t)
+        whole = pl.ds(0, W)
+        mix_in(t, whole, s.spec_mate[t], 2, False)
 
     def inner_back(t):
         hi, lo = parted(s.mixed[t] * s.scale_out[...])
         both = jnp.concatenate([hi, lo], axis=1)
-        size = G // 2 * C
+        size = NP // 2 * CP
         first = 1 - me // (G // 2)
         for turn in range(2):
             side = first if turn == 0 else 1 - first
@@ -465,49 +486,72 @@
                 wide = dot(s.turned[0, at, :], both)
                 s.send3[t, part, pl.ds(pl.multiple_of(side * size, 8), size), :] = (
                     wide[:, :L] + (wide[:, L:] + dot(s.turned[1, at, :], hi)))
-            for d, e in STEPS:
-                def make(d=d, e=e):
-                    to = to_dev(d, e)
-                    return remote(s.send3.at[t, :, rows(to), :], s.got3.at[t, me],
-                                  s.s3.at[t], s.r3.at[t, core], (band, to))
-                launch(make, to_dev(d, e) // (G // 2) == side)
-        sent(chunks(t, G - 1), s.s3.at[t])
-        s.got3[t, me] = s.send3[t, :, rows(me), :]
+            for h in range(len(plan.pieces[0])):
+                for d in list(range(1, NP)) + [0]:
+                    for c in range(2):
+                        start, count = plan.pieces[c][h]
+
+                        def make(d=d, c=c, start=start, count=count):
+                            to = 2 * ((pair + d) % NP) + c
+                            return remote(
+                                s.send3.at[t, :, piece_rows(to, start, count), :],
+                                s.got3.at[t, me, :, pl.ds(start, count), :],
+                                s.s3.at[t], s.r3.at[t, core, h], (band, to))
+                        here = (2 * ((pair + d) % NP)) // (G // 2) == side
+                        launch(make, here if d else here & (core != c))
+
+        def move(size):
+            s.got3[t, me, :, :size, :] = s.send3[t, :, piece_rows(me, 0, size), :]
+
+        own_of(lambda size: s.send3.at[t, :, pl.ds(0, used - size)], s.s3.at[t], move)
 
     def outer_back(t, g, edges):
-        recv_all(chunks(t, NP), s.r3.at[t, g], core != g)
-        recv_all(chunks(t, NP - 1), s.r3.at[t, g], core == g)
-
-        def step(index):
-            at = span(index, 8)
-            values = [s.got3[t, 2 * (row // 2) + g, row % 2, at, :] for row in range(G)]
-            for place in range(G):
-                s.send4[t, place, g, at, :] = weighted(values, table[:, place])
-
-        loop(C // 8, step)
-        for d, e in STEPS:
-            to = to_dev(d, e)
-            remote(s.send4.at[t, to, g], s.got4.at[t, g, rows(me), :],
-                   s.s4.at[t, g], s.r4.at[t, g], (band, to)).start()
-        sent(s.got1.at[t, g, pl.ds(0, G - 1)], s.s4.at[t, g])
-        s.got4[t, g, rows(me), :] = s.send4[t, me, g]
-        if not edges:
-            return
-        for way, (owner, shift, at) in enumerate((
-            (0, 1, 0), (last_chunk, G - 1, (length - 1) % C // 8 * 8))):
-            @pl.when(me == owner)
-            def _(way=way, shift=shift, at=at):
+        for h in range(len(plan.pieces[0])):
+            for c in range(2):
+                recv_all(s.got3.at[t, pl.ds(0, NP - (c == g)), :, pl.ds(0, plan.pieces[c][h][1]), :],
+                         s.r3.at[t, g, h], core == c)
+
+            def work(c):
+                start, count = plan.pieces[c][h]
+
+                def step(index):
+                    at = pl.ds(pl.multiple_of(index * 8 + start, 8), 8)
+                    values = [s.got3[t, 2 * (row // 2) + g, row % 2, at, :] for row in range(G)]
+                    for place in range(G):
+                        s.send4[t, place, g, at, :] = weighted(values, table[:, place])
+
+                loop(count // 8, step)
+                for way, (owner, shift, at) in enumerate(((0, 1, 0), (last_chunk, G - 1, last_at))):
+                    if not edges or owner % 2 != c or not start <= at < start + count:
+                        continue
+
+                    @pl.when(me == owner)
+                    def _(way=way, shift=shift, at=at):
+                        for d, e in STEPS:
+                            to = to_dev(d, e)
+                            remote(s.send4.at[t, (to + shift) % G, g, pl.ds(at, 8), :],
+                                   s.ew.at[way, g], s.sw.at[way], s.rw.at[way], (band, to)).start()
+                        s.ew[way, g] = s.send4[t, (me + shift) % G, g, pl.ds(at, 8), :]
+
                 for d, e in STEPS:
                     to = to_dev(d, e)
-                    remote(s.send4.at[t, (to + shift) % G, g, pl.ds(at, 8), :], s.ew.at[way, g],
-                           s.sw.at[way], s.rw.at[way], (band, to)).start()
-                s.ew[way, g] = s.send4[t, (me + shift) % G, g, pl.ds(at, 8), :]
-
-            if g == 1:
+                    remote(s.send4.at[t, to, g, pl.ds(start, count), :],
+                           s.got4.at[t, g, piece_rows(me, start, count), :],
+                           s.s4.at[t, g], s.r4.at[t, g], (band, to)).start()
+
+            for_core(work)
+
+        def move(size):
+            s.got4[t, g, piece_rows(me, 0, size), :] = s.send4[t, me, g, :size, :]
+
+        own_of(lambda size: s.got1.at[t, g, pl.ds(0, G - 1), pl.ds(0, size)], s.s4.at[t, g], move)
+        if edges and g == 1:
+            for way, owner in enumerate((0, last_chunk)):
                 sent(s.red1.at[0, pl.ds(0, G - 1)], s.sw.at[way], me == owner)
 
     def wait_back(t, g):
-        recv_all(s.got1.at[t, g, pl.ds(0, G - 1)], s.r4.at[t, g])
+        for c in range(2):
+            recv_all(s.xs.at[t, g, pl.ds(0, used - sizes[c])], s.r4.at[t, g], core == c)
 
     def wait_rows():
         for way, owner in enumerate((0, last_chunk)):
@@ -622,6 +666,11 @@
                 s.zgot[i, way] = jnp.zeros((PD, L), f32)
             s.zonal_in[way] = jnp.zeros((1, 2 * L), f32)
 
+    if PD > used:
+        for t in range(2):
+            s.cells[t, 0, :, used:, :] = jnp.zeros((2, PD - used, L), f32)
+            s.zgot[t, :, used:, :] = jnp.zeros((2, PD - used, L), f32)
+
     @pl.when(jnp.logical_not(has_down))
     def _():
         s.carried[...] = jnp.zeros((L, L), f32)
@@ -647,7 +696,6 @@
     is_low = core == 0
     zones = (
         jnp.where(is_low, zone_a, zone_b),
-        jnp.where(is_low, zone_b, zone_a),
         jnp.where(mask1, s.zonal_in[0, :, :L], s.zonal_in[1, :, L:]),
     )
 
@@ -685,12 +733,12 @@
         is_low, mid + pick((tl, al1), (br, al0)), pick((tl, al0 + low), (br, al1 + top)))
     beside = jnp.where(is_low, pick((tr, al0), (bl, al1)), pick((tr, al1), (bl, al0)))
     across = pick((tr, top), (bl, low))
-    for k, value in enumerate((own, beside, across)):
+    for k, value in enumerate((own, across, beside)):
         hi, lo = parted(value)
-        s.gain[k, :, :L] = hi
-        s.gain[k, :, L:] = lo
-
-    inner_forward(0, 0)
+        s.gain[k * L : (k + 1) * L, :L] = hi
+        s.gain[k * L : (k + 1) * L, L:] = lo
+
+    inner_forward(0)
     inner_back(0)
 
     def rz_part(index, carry):
@@ -741,12 +789,12 @@
                 (s.east[k, at8, :] + s.east[k, at7, :]) + (s.north[k, at, :] + s.south[k, at, :]))
     s.diag[:, length:R, :] = jnp.zeros((2, R - length, L), f32)
     loop_rows(make_diag)
-    if R > PD:
-        for t in range(2):
-            for g in range(2):
-                s.got4[t, g, PD:, :] = jnp.zeros((R - PD, L), f32)
-
-    drain()
+    for t in range(2):
+        for g in range(2):
+            if R > used:
+                s.got4[t, g, used:, :] = jnp.zeros((R - used, L), f32)
+
+    drain(2)
     outer_back(0, 0, True)
     outer_back(0, 1, True)
     wait_back(0, 0)
@@ -797,6 +845,7 @@
         s.xs[1, 0, at, :], s.xs[1, 1, at, :] = groups_of(*image)
 
     send_phase1(1, 0)
+    drain(2)
     wait_edges(1)
     north_col, south_col = column_of(1, 0), column_of(1, 1)
     for b in range(blocks):
@@ -810,12 +859,11 @@
     send_phase1(1, 1)
     s.part[0, 1] = curvature
     reduce_send(0)
-    drain()
 
     outer_forward(1, 0)
     outer_forward(1, 1)
     reduce_middle(0)
-    inner_forward(1, 1)
+    inner_forward(1)
     inner_back(1)
     rz_now, bend = reduce_end(0)
     alpha = rz_now / bend
@@ -830,10 +878,10 @@
     s.part[1, 1] = jnp.zeros((8, L), f32)
     reduce_send(1)
 
-    drain()
+    drain(3)
     outer_back(1, 0, False)
+    outer_back(1, 1, False)
     reduce_middle(1)
-    outer_back(1, 1, False)
 
     def first_outputs(start, count):
         at, at8 = pl.ds(start, count), eight_on(start, count)

time: 81.6 us -> 77.4 us (0.949)
  Pallas kernels: 80.6 us -> 76.6 us
    pallas_call x1, Pallas kernels: 78.3 us -> 74.3 us  [local(): pl.pallas_call(functools.partial(kernel, plan, tuple(scratch)), out_shape...]
where the time goes in v2:
time: 77.4 us; the launch traced here: 77.3 us
  Pallas kernels  76.6 us (99%)
    pallas_call x1, Pallas kernels, local(): pl.pallas_call(functools.partial(kernel, plan, tuple(scratch)), out_shape...  74.3 us
    pallas_call x1, Pallas kernels, local(): pl.pallas_call(finish_kernel, out_shape=(shape,) * 3, in_specs=[anywhere]...  2.28 us

profile of v2, /device:TPU:0, one launch (start us, length us, event | category | flops | bytes accessed | tf_op | source)
XLA Modules:
  0.0 77.3 jit_solution(10078196850629419115)
XLA Ops:
  0.6 74.3 %step.1 = (f32[540,256]{1,0:T(8,128)}, f32[540,256]{1,0:T(8,128)}, f32[540,256]{1,0:T(8,128)}) custom-call(f32[540,256]{1,0:T(8,128)} %refs_0_.1, s32[540,256]{1,0:T(8,128)} %refs_1_.1, f32[540,256]{1,0:T(8,128)} %refs_2_.1, f32[540,256]{1,0:T(8,128)} %refs_3_.1, f32[540,256]{1,0:T(8,128)} %refs_4_.1, f32[1,256]{1,0:T(1,128)} %bitcast.1, ...), custom_call_target="tpu_custom_call" | custom-call | tf_op jit(solution)/shard_map/step/pallas_call | solution.py:960
  75.0 2.3 %finish.1 = (f32[540,256]{1,0:T(8,128)}, f32[540,256]{1,0:T(8,128)}, f32[540,256]{1,0:T(8,128)}) custom-call(f32[540,256]{1,0:T(8,128)} %get-tuple-element.6.refs_0_, f32[540,256]{1,0:T(8,128)} %get-tuple-element.7.refs_1_, f32[540,256]{1,0:T(8,128)} %get-tuple-element.8.refs_2_), custom_call_target="tpu_custom_call" | custom-call | tf_op jit(solution)/shard_map/finish/pallas_call | solution.py:975

commit v3 on v2

--- a/solution.py
+++ b/solution.py
@@ -210,7 +210,12 @@
     mate = me + 1 - 2 * core
     has_up, has_down = band < bands - 1, band > 0
     sends_up, sends_down = (core == 1) & has_up, (core == 1) & has_down
-    STEPS = [(d, e) for d in range(1, NP) for e in (0, 1)] + [(0, 1)]
+    if NP == 4:
+        across_both = (2 * NP - 1 - 2 * pair) % NP
+        OTHERS = [across_both, NP - across_both, 2]
+    else:
+        OTHERS = list(range(1, NP))
+    STEPS = [(d, e) for d in OTHERS for e in (0, 1)] + [(0, 1)]
     CP, sizes = plan.pair_size, plan.sizes
     used = NP * CP
     last_pair, last_at = (length - 1) // CP, (length - 1) % CP
@@ -349,16 +354,16 @@
 
     def send_phase1(t, g):
         for h in range(len(pieces[t][0])):
-            for d in list(range(1, NP)) + [0]:
+            for d in OTHERS + [None]:
                 for c in range(2):
                     start, count = pieces[t][c][h]
 
                     def make(d=d, c=c, start=start, count=count):
-                        to = 2 * ((pair + d) % NP) + c
+                        to = 2 * (pair if d is None else (pair + d) % NP) + c
                         return remote(s.xs.at[t, g, piece_rows(to, start, count)],
                                       s.got1.at[t, g, me, pl.ds(start, count)],
                                       s.s1.at[t, g], s.r1.at[t, g, h], (band, to))
-                    launch(make, None if d else core != c)
+                    launch(make, core != c if d is None else None)
 
         def move(size):
             s.got1[t, g, me, :size, :] = s.xs[t, g, piece_rows(me, 0, size), :]
@@ -382,7 +387,7 @@
                         s.send2[t, row // 2, g, row % 2, at, :] = weighted(values, table[row])
 
                 loop(count // 8, step)
-                for d in list(range(1, NP)) + ([] if c == g else [0]):
+                for d in OTHERS + ([] if c == g else [0]):
                     to = (pair + d) % NP
                     remote(s.send2.at[t, to, g, :, pl.ds(start, count), :],
                            s.cells.at[t, 0, :, piece_rows(me, start, count), :],
@@ -474,7 +479,7 @@
         whole = pl.ds(0, W)
         mix_in(t, whole, s.spec_mate[t], 2, False)
 
-    def inner_back(t):
+    def inner_back(t, between=None):
         hi, lo = parted(s.mixed[t] * s.scale_out[...])
         both = jnp.concatenate([hi, lo], axis=1)
         size = NP // 2 * CP
@@ -487,18 +492,21 @@
                 s.send3[t, part, pl.ds(pl.multiple_of(side * size, 8), size), :] = (
                     wide[:, :L] + (wide[:, L:] + dot(s.turned[1, at, :], hi)))
             for h in range(len(plan.pieces[0])):
-                for d in list(range(1, NP)) + [0]:
+                for d in OTHERS + [None]:
                     for c in range(2):
                         start, count = plan.pieces[c][h]
 
                         def make(d=d, c=c, start=start, count=count):
-                            to = 2 * ((pair + d) % NP) + c
+                            to = 2 * (pair if d is None else (pair + d) % NP) + c
                             return remote(
                                 s.send3.at[t, :, piece_rows(to, start, count), :],
                                 s.got3.at[t, me, :, pl.ds(start, count), :],
                                 s.s3.at[t], s.r3.at[t, core, h], (band, to))
-                        here = (2 * ((pair + d) % NP)) // (G // 2) == side
-                        launch(make, here if d else here & (core != c))
+                        target = pair if d is None else (pair + d) % NP
+                        here = target // (NP // 2) == side
+                        launch(make, here & (core != c) if d is None else here)
+            if between is not None and turn == 0:
+                between()
 
         def move(size):
             s.got3[t, me, :, :size, :] = s.send3[t, :, piece_rows(me, 0, size), :]
@@ -864,7 +872,6 @@
     outer_forward(1, 1)
     reduce_middle(0)
     inner_forward(1)
-    inner_back(1)
     rz_now, bend = reduce_end(0)
     alpha = rz_now / bend
 
@@ -874,9 +881,12 @@
         mixed = s.mixed[0, at, :] - alpha * s.mixed[1, at, :]
         return carry + eights(spectrum * (mixed * weight_of(at)))
 
-    s.part[1, 0] = lax.fori_loop(0, W // 128, rz_next_part, jnp.zeros((8, L), f32))
-    s.part[1, 1] = jnp.zeros((8, L), f32)
-    reduce_send(1)
+    def send_rz_next():
+        s.part[1, 0] = lax.fori_loop(0, W // 128, rz_next_part, jnp.zeros((8, L), f32))
+        s.part[1, 1] = jnp.zeros((8, L), f32)
+        reduce_send(1)
+
+    inner_back(1, send_rz_next)
 
     drain(3)
     outer_back(1, 0, False)

time: 77.4 us -> 76.8 us (level)
  no operation moved by 1% of the time
where the time goes in v3:
time: 76.8 us; the launch traced here: 76.6 us
  Pallas kernels  76 us (99%)
    pallas_call x1, Pallas kernels, local(): pl.pallas_call(functools.partial(kernel, plan, tuple(scratch)), out_shape...  73.7 us
    pallas_call x1, Pallas kernels, local(): pl.pallas_call(finish_kernel, out_shape=(shape,) * 3, in_specs=[anywhere]...  2.28 us

profile of v3, /device:TPU:0, one launch (start us, length us, event | category | flops | bytes accessed | tf_op | source)
XLA Modules:
  0.0 76.6 jit_solution(10784232655695208442)
XLA Ops:
  0.6 73.7 %step.1 = (f32[540,256]{1,0:T(8,128)}, f32[540,256]{1,0:T(8,128)}, f32[540,256]{1,0:T(8,128)}) custom-call(f32[540,256]{1,0:T(8,128)} %refs_0_.1, s32[540,256]{1,0:T(8,128)} %refs_1_.1, f32[540,256]{1,0:T(8,128)} %refs_2_.1, f32[540,256]{1,0:T(8,128)} %refs_3_.1, f32[540,256]{1,0:T(8,128)} %refs_4_.1, f32[1,256]{1,0:T(1,128)} %bitcast.1, ...), custom_call_target="tpu_custom_call" | custom-call | tf_op jit(solution)/shard_map/step/pallas_call | solution.py:970
  74.4 2.3 %finish.1 = (f32[540,256]{1,0:T(8,128)}, f32[540,256]{1,0:T(8,128)}, f32[540,256]{1,0:T(8,128)}) custom-call(f32[540,256]{1,0:T(8,128)} %get-tuple-element.6.refs_0_, f32[540,256]{1,0:T(8,128)} %get-tuple-element.7.refs_1_, f32[540,256]{1,0:T(8,128)} %get-tuple-element.8.refs_2_), custom_call_target="tpu_custom_call" | custom-call | tf_op jit(solution)/shard_map/finish/pallas_call | solution.py:985
